TPU v7x, 32 devices: a whole 2x2x4 slice. The times are simulated.
32 devices in a mesh: comp: 2 (over core), lat: 4 (over z), lon: 4 (over y, x).
Axes of the slice: x: 2, y: 2, z: 4, core: 2. Of those that a mesh axis runs over, the one named last changes fastest.
Arguments:
- fields: float32 [2, 7, 2048, 256], P('comp', None, ('lat', 'lon')), may hold values from -4 to 4, as said below
- block_owner: int32 [2048], P(('lat', 'lon')), may hold values from 0 to 2047, as said below
- ice_covered: int32 [2048], P(('lat', 'lon')), may hold values 0 or 1
- land_mask: int32 [2048, 256], P(('lat', 'lon')), may hold values 0 or 1
Outputs:
- coupled_out: float32 [2, 2, 2048, 256], P('comp', None, ('lat', 'lon'))
Inputs may be any that keep to these rules, and one draw needn't show every extreme that they name: `block_owner`: every block id appears once. Slot d of lat+lon index o holds a block of the ice tile of index d, that is an id from d * 128 to d * 128 + 127. `fields`: ocean channels: winds within 4, currents within 1.5, tilts within 1, air density 0.9 to 1.3; ice channels: velocities within 1.5, mass 0.5 to 4, concentration 0.05 to 1, stresses within 1.5.
All inputs are finite; a program needn't handle non-finite values.
Results may differ from a plain program's by a relative error of at most 0.00002.
Values sent between devices are 32-bit elements.
A program may use at most 64 MiB of HBM per device.

v0:
```python
import functools

import jax
import jax.numpy as jnp
from jax import lax
from jax.experimental import pallas as pl
from jax.experimental.pallas import tpu as pltpu
from jax.sharding import PartitionSpec as P

GX = 1
BY = 2
BX = 128
NSUB = 4


CD_ICE = 0.1
CW = 1.5
CSTAR = 2.0
ECC2 = 4.0
DMIN2 = 0.25
RELAX = 0.5
DTE = 0.5
CORIO = 0.3
MASS_FLOOR = 0.5
DRAG_FLOOR = 0.1


def from_behind(x, axis, by):
    size = lax.axis_size(axis)
    pairs = [(i, i + by) for i in range(size) if 0 <= i + by < size]
    return lax.ppermute(x, axis, pairs)


def with_halo(x, sides, width, wrap):
    for axis, dim in sides:
        size, length = (lax.axis_size(axis), x.shape[dim])
        up = [(i, (i + 1) % size) for i in range(size if wrap else size - 1)]
        down = [(j, i) for i, j in up]
        last = lax.slice_in_dim(x, length - width, length, axis=dim)
        first = lax.slice_in_dim(x, 0, width, axis=dim)
        before = lax.ppermute(last, axis, up)
        after = lax.ppermute(first, axis, down)
        x = jnp.concatenate([before, x, after], axis=dim)
    return x


def air_stress(ocean):
    wind_x, wind_y, current_x, current_y, tilt_x, tilt_y, density = ocean
    speed_ice = jnp.sqrt(wind_x * wind_x + wind_y * wind_y + 1.0)
    scale_ice = density * CD_ICE * speed_ice
    rel_x = wind_x - current_x
    rel_y = wind_y - current_y
    speed_open = jnp.sqrt(rel_x * rel_x + rel_y * rel_y + 1.0)
    scale_open = density * (0.1 + 0.05 * speed_open) * speed_open
    outbound = jnp.stack(
        [scale_ice * wind_x, scale_ice * wind_y, current_x, current_y, tilt_x, tilt_y]
    )
    open_stress = jnp.stack([scale_open * rel_x, scale_open * rel_y])
    return (outbound, open_stress)


def prepare(ice_tile, forcing, active):
    ice_mass = ice_tile[2]
    concentration = ice_tile[3]
    strength = ice_mass * jnp.exp(CSTAR * (concentration - 1.0)) * active
    drag_base = CW * concentration * active
    push_x = active * (concentration * forcing[0] - ice_mass * forcing[4])
    push_y = active * (concentration * forcing[1] - ice_mass * forcing[5])
    return jnp.stack(
        [strength, ice_mass, drag_base, push_x, push_y, forcing[2], forcing[3], active]
    )


def subcycle(ice_state, statics):
    east_vel, north_vel, stress_one, stress_two, stress_three = ice_state
    strength = statics[0]
    east_base = east_vel[:-1, :-1]
    north_base = north_vel[:-1, :-1]
    strain_xx = east_vel[:-1, 1:] - east_base
    strain_yy = north_vel[1:, :-1] - north_base
    shear = east_vel[1:, :-1] - east_base + (north_vel[:-1, 1:] - north_base)
    divergence = strain_xx + strain_yy
    tension = strain_xx - strain_yy
    delta_norm = jnp.sqrt(
        divergence * divergence + (tension * tension + shear * shear) / ECC2 + DMIN2
    )
    viscosity = strength[:-1, :-1] / delta_norm
    stress_sum = (stress_one[:-1, :-1] + RELAX * viscosity * (divergence - delta_norm)) / (
        1.0 + RELAX
    )
    stress_diff = (stress_two[:-1, :-1] + RELAX * viscosity * tension / ECC2) / (1.0 + RELAX)
    stress_shear = (stress_three[:-1, :-1] + RELAX * viscosity * shear / (2.0 * ECC2)) / (
        1.0 + RELAX
    )
    stress_xx = 0.5 * (stress_sum + stress_diff)
    stress_yy = 0.5 * (stress_sum - stress_diff)
    force_x = (
        stress_xx[1:, 1:] - stress_xx[1:, :-1] + (stress_shear[1:, 1:] - stress_shear[:-1, 1:])
    )
    force_y = (
        stress_shear[1:, 1:] - stress_shear[1:, :-1] + (stress_yy[1:, 1:] - stress_yy[:-1, 1:])
    )
    trimmed = statics[:, 1:-1, 1:-1]
    strength, ice_mass, drag_base, push_x, push_y, current_x, current_y, active = trimmed
    east_old = east_vel[1:-1, 1:-1]
    north_old = north_vel[1:-1, 1:-1]
    diff_x = current_x - east_old
    diff_y = current_y - north_old
    drag_coef = drag_base * jnp.sqrt(diff_x * diff_x + diff_y * diff_y + DRAG_FLOOR)
    denominator = jnp.maximum(ice_mass, MASS_FLOOR) / DTE + drag_coef
    east_new = (
        active
        * (
            ice_mass / DTE * east_old
            + force_x
            + push_x
            + drag_coef * current_x
            + CORIO * ice_mass * north_old
        )
        / denominator
    )
    north_new = (
        active
        * (
            ice_mass / DTE * north_old
            + force_y
            + push_y
            + drag_coef * current_y
            - CORIO * ice_mass * east_old
        )
        / denominator
    )
    new_state = jnp.stack(
        [east_new, north_new, stress_sum[1:, 1:], stress_diff[1:, 1:], stress_shear[1:, 1:]]
    )
    return (new_state, trimmed)


def give_back(ice_state, statics):
    east_vel = ice_state[0]
    north_vel = ice_state[1]
    drag_base = statics[2]
    current_x = statics[5]
    current_y = statics[6]
    diff_x = east_vel - current_x
    diff_y = north_vel - current_y
    factor = drag_base * jnp.sqrt(diff_x * diff_x + diff_y * diff_y + DRAG_FLOOR)
    return jnp.stack([factor * diff_x, factor * diff_y, drag_base / CW])


def to_tile(blocks):
    channels, count, cells = blocks.shape
    arranged = blocks.reshape(channels, count // GX, GX, BY, BX).transpose(0, 1, 3, 2, 4)
    return arranged.reshape(channels, count // GX * BY, GX * BX)


def from_tile(values):
    channels, rows, columns = values.shape
    arranged = values.reshape(channels, rows // BY, BY, GX, BX).transpose(0, 1, 3, 2, 4)
    return arranged.reshape(channels, rows // BY * GX, BY * BX)


def per_device(fields, block_owner, ice_covered, land_mask):
    count = block_owner.shape[0]
    is_ocean = lax.axis_index("comp") == 0
    outbound, open_stress = air_stress(fields[0])
    owner_row = block_owner.reshape(1, count)
    crossed = from_behind(outbound, "comp", 1)
    received, anchor = (
        lax.all_to_all(crossed, ("lat", "lon"), split_axis=1, concat_axis=1, tiled=True),
        lax.all_to_all(owner_row, ("lat", "lon"), split_axis=1, concat_axis=1, tiled=True),
    )
    local_ids = anchor[0] % count
    position = jnp.zeros((count,), jnp.int32).at[local_ids].set(jnp.arange(count, dtype=jnp.int32))
    forcing = to_tile(received[:, position])
    ice_tile = to_tile(fields[0])
    covered = ice_covered.astype(jnp.float32)[:, None] * (1 - land_mask).astype(jnp.float32)
    active = to_tile(covered[None])[0]
    statics = prepare(ice_tile, forcing, active)
    ice_state = jnp.stack([ice_tile[0], ice_tile[1], ice_tile[4], ice_tile[5], ice_tile[6]])
    joined = jnp.concatenate([ice_state, statics], 0)
    joined = with_halo(joined, (("lon", 2),), NSUB, True)
    joined = with_halo(joined, (("lat", 1),), NSUB, False)
    ice_state = joined[:5]
    statics = joined[5:]
    for repeat in range(NSUB):
        ice_state, statics = subcycle(ice_state, statics)
    returned = from_tile(give_back(ice_state, statics))
    back_send = returned[:, local_ids]
    regrouped = lax.all_to_all(back_send, ("lat", "lon"), split_axis=1, concat_axis=1, tiled=True)
    received_back = from_behind(regrouped, "comp", -1)
    ocean_out = received_back[:2] + (1.0 - received_back[2]) * open_stress
    ice_out = from_tile(ice_state[:2])
    return jnp.where(is_ocean, ocean_out, ice_out)[None]


LEAD = 16
GROUP = 6
TILE = 8
MESH = pl.DeviceIdType.MESH
DIRECTIONS = [(a, b) for a in (-1, 0, 1) for b in (-1, 0, 1) if (a, b) != (0, 0)]
U, V, MASS, CONC, S1, S2, S12, ACTIVE, PUSH_X, PUSH_Y, CUR_X, CUR_Y = range(12)


def tile_loop(tiles, together, body):
    def step(k, carry):
        for j in range(together):
            body(k * together + j)
        return carry
    lax.fori_loop(0, tiles // together, step, 0)


def split_dot(one_hot, values, contract):
    total = None
    rest = values
    for piece in range(3):
        part = rest.astype(jnp.bfloat16)
        if piece < 2:
            rest = rest - part.astype(jnp.float32)
        term = lax.dot_general(
            one_hot, part, ((contract, (0,)), ((), ())), preferred_element_type=jnp.float32
        )
        total = term if total is None else total + term
    return total


def step_kernel(
    n_lat, n_lon,
    fields, owner, covered, land, out,
    surf, open_st, ret, ids, recv, grid, strength, dragb, forc, one_hot, back, land_v,
    pack_early, pack_mid, pack_late, got_early, got_mid, got_late,
    load_sem, ids_ssem, ids_rsem, fwd_ssem, fwd_rsem, ret_ssem, ret_rsem,
    early_ssem, early_rsem, mid_ssem, mid_rsem, late_ssem, late_rsem,
):
    comp = lax.axis_index("comp")
    lat = lax.axis_index("lat")
    lon = lax.axis_index("lon")
    peers = n_lat * n_lon
    me = lat * n_lon + lon
    count = owner.shape[1]
    per = count // peers
    width = BX
    barrier = pltpu.get_barrier_semaphore()

    def rows_of(peer):
        return pl.ds(pl.multiple_of(peer * per, per), per)

    def device(kind, peer):
        return (kind, peer // n_lon, peer % n_lon)

    def each_peer(body):
        def step(k, carry):
            body((me + k) % peers)
            return carry
        lax.fori_loop(0, peers, step, 0)

    def signal_peers(kind):
        each_peer(
            lambda p: pl.semaphore_signal(
                barrier, inc=1, device_id=device(kind, p), device_id_type=MESH
            )
        )

    def send_rows(kind, src, lo, num, dst, dlo, ssem, rsem):
        def body(p):
            pltpu.make_async_remote_copy(
                src_ref=src.at[pl.ds(lo, num), rows_of(p), :],
                dst_ref=dst.at[pl.ds(dlo, num), rows_of(me), :],
                send_sem=ssem, recv_sem=rsem,
                device_id=device(kind, p), device_id_type=MESH,
            ).start()
        each_peer(body)

    def wait_bytes(ref, sem):
        pltpu.make_async_copy(ref, ref, sem).wait()

    @pl.when(comp == 0)
    def _ocean():
        signal_peers(1)
        raw = pltpu.make_async_copy(fields.at[0, pl.ds(2, 4)], surf.at[pl.ds(2, 4)], load_sem.at[0])
        wind = pltpu.make_async_copy(fields.at[0, pl.ds(0, 2)], surf.at[pl.ds(0, 2)], load_sem.at[1])
        rho = pltpu.make_async_copy(fields.at[0, pl.ds(6, 1)], surf.at[pl.ds(6, 1)], load_sem.at[2])
        raw.start()
        wind.start()
        rho.start()
        pl.semaphore_wait(barrier, peers)

        def ids_out(p):
            pltpu.make_async_remote_copy(
                src_ref=owner, dst_ref=ids.at[me], send_sem=ids_ssem, recv_sem=ids_rsem,
                device_id=device(1, p), device_id_type=MESH,
            ).start()
        each_peer(ids_out)
        raw.wait()
        send_rows(1, surf, 2, 4, recv, 2, fwd_ssem.at[0], fwd_rsem.at[0])
        wind.wait()
        rho.wait()

        def stress(t):
            r = pl.ds(pl.multiple_of(t * TILE, TILE), TILE)
            wx, wy, density = surf[0, r, :], surf[1, r, :], surf[6, r, :]
            scale = density * CD_ICE * jnp.sqrt(wx * wx + wy * wy + 1.0)
            forc[0, r, :] = scale * wx
            forc[1, r, :] = scale * wy

        tile_loop(count // TILE, 2, stress)
        send_rows(1, forc, 0, 2, recv, 0, fwd_ssem.at[1], fwd_rsem.at[1])

        def open_water(t):
            r = pl.ds(pl.multiple_of(t * TILE, TILE), TILE)
            density = surf[6, r, :]
            rel_x = surf[0, r, :] - surf[2, r, :]
            rel_y = surf[1, r, :] - surf[3, r, :]
            speed = jnp.sqrt(rel_x * rel_x + rel_y * rel_y + 1.0)
            scale = density * (0.1 + 0.05 * speed) * speed
            open_st[0, r, :] = scale * rel_x
            open_st[1, r, :] = scale * rel_y

        tile_loop(count // TILE, 2, open_water)
        wait_bytes(ret.at[pl.ds(2, 1)], ret_rsem.at[0])
        wait_bytes(ret.at[pl.ds(0, 2)], ret_rsem.at[1])

        def finish(t):
            r = pl.ds(pl.multiple_of(t * TILE, TILE), TILE)
            water = 1.0 - ret[2, r, :]
            out[0, 0, r, :] = ret[0, r, :] + water * open_st[0, r, :]
            out[0, 1, r, :] = ret[1, r, :] + water * open_st[1, r, :]

        tile_loop(count // TILE, 2, finish)
        wait_bytes(ids, ids_ssem)
        wait_bytes(surf.at[pl.ds(2, 4)], fwd_ssem.at[0])
        wait_bytes(forc.at[pl.ds(0, 2)], fwd_ssem.at[1])

    @pl.when(comp == 1)
    def _ice():
        def inside(a):
            if a == 0:
                return lat >= 0
            return lat + a >= 0 if a < 0 else lat + a < n_lat

        signal_peers(0)
        first, last = LEAD, LEAD + count
        core = pl.ds(first, count)
        main, side = pl.ds(0, width), pl.ds(width, width)
        loads = [
            pltpu.make_async_copy(
                fields.at[0, :, :, pl.ds(y * width, width)],
                grid.at[pl.ds(0, 7), y, core, main],
                load_sem.at[y],
            )
            for y in range(2)
        ]
        loads.append(pltpu.make_async_copy(land, land_v, load_sem.at[2]))
        for load in loads:
            load.start()
        for c in range(12):
            for y in range(2):
                blank = jnp.zeros((LEAD, 2 * width), jnp.float32)
                grid[c, y, pl.ds(0, LEAD), :] = blank
                grid[c, y, pl.ds(last, LEAD), :] = blank
        for got in (got_early, got_mid, got_late):
            for d in range(2):
                got[d, pl.ds(0, TILE), :] = jnp.zeros((TILE, width), jnp.float32)
                got[d, pl.ds(TILE + count, TILE), :] = jnp.zeros((TILE, width), jnp.float32)

        for a, b in DIRECTIONS:
            @pl.when(inside(a))
            def _():
                pl.semaphore_signal(
                    barrier, inc=1, device_id=(1, lat + a, (lon + b + n_lon) % n_lon),
                    device_id_type=MESH,
                )
        walls = jnp.where(lat == 0, 3, 0) + jnp.where(lat == n_lat - 1, 3, 0)
        pl.semaphore_wait(barrier, peers + 8 - walls)
        for load in loads:
            load.wait()

        diag = lax.broadcasted_iota(jnp.int32, (count, count), 0) == lax.broadcasted_iota(
            jnp.int32, (count, count), 1
        )
        wet = jnp.sum(
            jnp.where(diag, covered[...].astype(jnp.float32), 0.0), axis=1, keepdims=True
        )
        sea = wet * (1 - land_v[...]).astype(jnp.float32)
        for y in range(2):
            grid[ACTIVE, y, core, main] = sea[:, y * width:(y + 1) * width]

        lane = lax.broadcasted_iota(jnp.int32, (TILE, width), 1)

        def pack(lo, num, packed):
            def body(t):
                r = pl.ds(pl.multiple_of(first + t * TILE, TILE), TILE)
                east = jnp.zeros((TILE, width), jnp.float32)
                west = east
                for c in range(num):
                    for y in range(2):
                        x = grid[lo + c, y, r, main]
                        slot = (c * 2 + y) * NSUB
                        mine = (lane >= slot) & (lane < slot + NSUB)
                        east = jnp.where(mine, pltpu.roll(x, (slot + NSUB) % width, 1), east)
                        west = jnp.where(mine, pltpu.roll(x, slot, 1) if slot else x, west)
                q = pl.ds(pl.multiple_of(t * TILE, TILE), TILE)
                packed[0, q, :] = east
                packed[1, q, :] = west
            tile_loop(count // TILE, 2, body)

        def halo(lo, num, packed, got, ssem, rsem, begin):
            for k, (a, b) in enumerate(DIRECTIONS):
                src_row = {-1: 0, 0: 0, 1: count - TILE}[a]
                dst_row = {-1: count, 0: 0, 1: -TILE}[a]
                rows = count if a == 0 else TILE
                if b == 0:
                    src = grid.at[pl.ds(lo, num), :, pl.ds(first + src_row, rows), main]
                    dst = grid.at[pl.ds(lo, num), :, pl.ds(first + dst_row, rows), main]
                else:
                    d = 0 if b > 0 else 1
                    src = packed.at[d, pl.ds(src_row, rows), :]
                    dst = got.at[d, pl.ds(TILE + dst_row, rows), :]
                copy = pltpu.make_async_remote_copy(
                    src_ref=src, dst_ref=dst, send_sem=ssem.at[k], recv_sem=rsem.at[k],
                    device_id=(1, lat + a, (lon + b + n_lon) % n_lon), device_id_type=MESH,
                )
                if begin:
                    @pl.when(inside(a))
                    def _():
                        copy.start()
                else:
                    @pl.when(inside(a))
                    def _():
                        copy.wait_send()

                    @pl.when(inside(-a))
                    def _():
                        copy.wait_recv()

        def side_of(got, slot, q):
            east = got[1, q, :]
            west = got[0, q, :]
            east = pltpu.roll(east, (width - slot) % width, 1) if slot else east
            west = pltpu.roll(west, width - NSUB - slot, 1)
            return jnp.where(
                lane < NSUB, east, jnp.where(lane >= width - NSUB, west, 0.0)
            )

        def unpack(lo, num, got, after):
            def body(t):
                q = pl.ds(pl.multiple_of(t * TILE, TILE), TILE)
                r = pl.ds(pl.multiple_of(first + (t - 1) * TILE, TILE), TILE)
                for c in range(num):
                    for y in range(2):
                        grid[lo + c, y, r, side] = side_of(got, (c * 2 + y) * NSUB, q)
                after(r)
            tile_loop(count // TILE + 2, 2, body)

        pack(0, 8, pack_early)
        halo(0, 8, pack_early, got_early, early_ssem, early_rsem, True)

        def ice_statics(r):
            for y in range(2):
                conc = grid[CONC, y, r, :]
                act = grid[ACTIVE, y, r, :]
                strength[y, r, :] = (
                    (RELAX / (1.0 + RELAX)) * grid[MASS, y, r, :] * jnp.exp(CSTAR * (conc - 1.0)) * act
                )
                dragb[y, r, :] = CW * conc * act

        wait_bytes(ids, ids_rsem)
        wanted = me * per
        row_lane = lax.broadcasted_iota(jnp.int32, (per, count), 1)
        row_sub = lax.broadcasted_iota(jnp.int32, (per, count), 0)
        mine = row_lane == row_sub + wanted
        blocks = lax.broadcasted_iota(jnp.int32, (per, count), 1).astype(jnp.float32)
        base = (me * count).astype(jnp.float32)
        for p in range(peers):
            owned = jnp.broadcast_to(ids[p], (per, count)).astype(jnp.float32)
            local = jnp.sum(jnp.where(mine, owned, 0.0), axis=1, keepdims=True) - base
            one_hot[pl.ds(p * per, per), :] = jnp.where(local == blocks, 1.0, 0.0)

        halo(0, 8, pack_early, got_early, early_ssem, early_rsem, False)
        unpack(0, 8, got_early, ice_statics)

        def east_of(x):
            return pltpu.roll(x, 2 * width - 1, 1)

        def west_of(x):
            return pltpu.roll(x, 1, 1)

        sub = lax.broadcasted_iota(jnp.int32, (TILE, 2 * width), 0)

        def next_row(x, after):
            return pltpu.roll(jnp.where(sub == 0, after, x), TILE - 1, 0)

        def last_row(x, before):
            return pltpu.roll(jnp.where(sub == TILE - 1, before, x), 1, 0)

        def sweep(g, new_stress, new_velocity):
            spots = [
                pl.ds(pl.multiple_of(first + (g * GROUP + j - 2) * TILE, TILE), TILE)
                for j in range(GROUP + 2)
            ]
            before, spots, after = spots[0], spots[1:-1], spots[-1]
            keep = 1.0 / (1.0 + RELAX)
            vels, stresses = [], []
            for r in spots:
                vels.append([(grid[U, y, r, :], grid[V, y, r, :]) for y in range(2)])
            if new_stress:
                follow = (grid[U, 0, after, :], grid[V, 0, after, :])
            for j, r in enumerate(spots):
                if not new_stress:
                    stresses.append(
                        [tuple(grid[c, y, r, :] for c in (S1, S2, S12)) for y in range(2)]
                    )
                    continue
                beyond = vels[j + 1][0] if j + 1 < GROUP else follow
                row = []
                for y in range(2):
                    u, v = vels[j][y]
                    if y == 0:
                        u_up, v_up = vels[j][1]
                    else:
                        u_up = next_row(vels[j][0][0], beyond[0])
                        v_up = next_row(vels[j][0][1], beyond[1])
                    sxx = east_of(u) - u
                    syy = v_up - v
                    shear = (u_up - u) + (east_of(v) - v)
                    div = sxx + syy
                    ten = sxx - syy
                    square = div * div + (ten * ten + shear * shear) * (1.0 / ECC2) + DMIN2
                    inverse = lax.rsqrt(square)
                    visc = strength[y, r, :] * inverse
                    s1 = grid[S1, y, r, :] * keep + visc * (div - square * inverse)
                    s2 = grid[S2, y, r, :] * keep + visc * ten * (1.0 / ECC2)
                    s12 = grid[S12, y, r, :] * keep + visc * shear * (0.5 / ECC2)
                    grid[S1, y, r, :] = s1
                    grid[S2, y, r, :] = s2
                    grid[S12, y, r, :] = s12
                    row.append((s1, s2, s12))
                stresses.append(row)
            if not new_velocity:
                return
            yy_before = 0.5 * (grid[S1, 1, before, :] - grid[S2, 1, before, :])
            cross_before = grid[S12, 1, before, :]
            for j, r in enumerate(spots):
                xx = [0.5 * (s1 + s2) for s1, s2, _ in stresses[j]]
                yy = [0.5 * (s1 - s2) for s1, s2, _ in stresses[j]]
                cross = [s12 for _, _, s12 in stresses[j]]
                yy_down = [last_row(yy[1], yy_before), yy[0]]
                cross_down = [last_row(cross[1], cross_before), cross[0]]
                yy_before, cross_before = yy[1], cross[1]
                for y in range(2):
                    u, v = vels[j][y]
                    force_x = xx[y] - west_of(xx[y]) + (cross[y] - cross_down[y])
                    force_y = cross[y] - west_of(cross[y]) + (yy[y] - yy_down[y])
                    mass = grid[MASS, y, r, :]
                    cx, cy = grid[CUR_X, y, r, :], grid[CUR_Y, y, r, :]
                    dx, dy = cx - u, cy - v
                    square = dx * dx + dy * dy + DRAG_FLOOR
                    drag = dragb[y, r, :] * (square * lax.rsqrt(square))
                    gain = grid[ACTIVE, y, r, :] / (
                        jnp.maximum(mass, MASS_FLOOR) * (1.0 / DTE) + drag
                    )
                    inertia = mass * (1.0 / DTE)
                    turn = CORIO * mass
                    grid[U, y, r, :] = gain * (
                        inertia * u + force_x + grid[PUSH_X, y, r, :] + drag * cx + turn * v
                    )
                    grid[V, y, r, :] = gain * (
                        inertia * v + force_y + grid[PUSH_Y, y, r, :] + drag * cy - turn * u
                    )

        groups = (count // TILE + 2) // GROUP

        def stress_only():
            tile_loop(groups, 1, lambda g: sweep(g, True, False))

        perm = one_hot[...].astype(jnp.bfloat16)
        stress_only()
        wait_bytes(recv.at[pl.ds(2, 4)], fwd_rsem.at[0])
        for c in range(2):
            both = split_dot(perm, recv[2 + c], (0,))
            for y in range(2):
                grid[CUR_X + c, y, core, main] = both[:, y * width:(y + 1) * width]
        pack(CUR_X, 2, pack_mid)
        halo(CUR_X, 2, pack_mid, got_mid, mid_ssem, mid_rsem, True)
        for c in range(2):
            both = split_dot(perm, recv[4 + c], (0,))
            for y in range(2):
                part = both[:, y * width:(y + 1) * width]
                grid[PUSH_X + c, y, core, main] = grid[MASS, y, core, main] * part
        wait_bytes(recv.at[pl.ds(0, 2)], fwd_rsem.at[1])
        for c in range(2):
            both = split_dot(perm, recv[c], (0,))
            for y in range(2):
                part = both[:, y * width:(y + 1) * width]
                grid[PUSH_X + c, y, core, main] = grid[ACTIVE, y, core, main] * (
                    grid[CONC, y, core, main] * part - grid[PUSH_X + c, y, core, main]
                )
        pack(PUSH_X, 2, pack_late)
        halo(PUSH_X, 2, pack_late, got_late, late_ssem, late_rsem, True)

        for y in range(2):
            share = grid[CONC, y, core, main] * grid[ACTIVE, y, core, main]
            back[2, :, pl.ds(y * width, width)] = split_dot(perm, share, (1,))
        send_rows(0, back, 2, 1, ret, 2, ret_ssem.at[0], ret_rsem.at[0])

        halo(CUR_X, 2, pack_mid, got_mid, mid_ssem, mid_rsem, False)
        unpack(CUR_X, 2, got_mid, lambda r: None)
        halo(PUSH_X, 2, pack_late, got_late, late_ssem, late_rsem, False)
        unpack(PUSH_X, 2, got_late, lambda r: None)
        tile_loop(groups, 1, lambda g: sweep(g, False, True))
        tile_loop((NSUB - 1) * groups, 1, lambda k: sweep(k % groups, True, True))

        def returned(t):
            q = pl.ds(pl.multiple_of(t * TILE, TILE), TILE)
            r = pl.ds(pl.multiple_of(first + t * TILE, TILE), TILE)
            for y in range(2):
                half = pl.ds(y * width, width)
                u, v = grid[U, y, r, main], grid[V, y, r, main]
                out[0, 0, q, half] = u
                out[0, 1, q, half] = v
                dx, dy = u - grid[CUR_X, y, r, main], v - grid[CUR_Y, y, r, main]
                drag = dragb[y, r, main] * jnp.sqrt(dx * dx + dy * dy + DRAG_FLOOR)
                forc[0, q, half] = drag * dx
                forc[1, q, half] = drag * dy

        tile_loop(count // TILE, 2, returned)
        for c in range(2):
            back[c] = split_dot(perm, forc[c], (1,))
        send_rows(0, back, 0, 2, ret, 0, ret_ssem.at[1], ret_rsem.at[1])
        wait_bytes(back.at[pl.ds(2, 1)], ret_ssem.at[0])
        wait_bytes(back.at[pl.ds(0, 2)], ret_ssem.at[1])


def per_device_kernel(n_lat, n_lon, fields, block_owner, ice_covered, land_mask):
    count, cells = land_mask.shape
    peers = n_lat * n_lon
    long = count + 2 * LEAD
    f32 = jnp.float32
    anywhere = pl.BlockSpec(memory_space=pl.ANY)
    in_vmem = pl.BlockSpec(memory_space=pltpu.VMEM)
    dma = pltpu.SemaphoreType.DMA
    return pl.pallas_call(
        functools.partial(step_kernel, n_lat, n_lon),
        out_shape=pltpu.VMEM((1, 2, count, cells), f32),
        in_specs=[anywhere, in_vmem, in_vmem, anywhere],
        out_specs=in_vmem,
        scratch_shapes=[
            pltpu.VMEM((7, count, cells), f32),
            pltpu.VMEM((2, count, cells), f32),
            pltpu.VMEM((3, count, cells), f32),
            pltpu.VMEM((peers, 1, count), jnp.int32),
            pltpu.VMEM((6, count, cells), f32),
            pltpu.VMEM((12, 2, long, 2 * BX), f32),
            pltpu.VMEM((2, long, 2 * BX), f32),
            pltpu.VMEM((2, long, 2 * BX), f32),
            pltpu.VMEM((6, count, cells), f32),
            pltpu.VMEM((count, count), f32),
            pltpu.VMEM((3, count, cells), f32),
            pltpu.VMEM((count, cells), jnp.int32),
            pltpu.VMEM((2, count, BX), f32),
            pltpu.VMEM((2, count, BX), f32),
            pltpu.VMEM((2, count, BX), f32),
            pltpu.VMEM((2, count + 2 * TILE, BX), f32),
            pltpu.VMEM((2, count + 2 * TILE, BX), f32),
            pltpu.VMEM((2, count + 2 * TILE, BX), f32),
            dma((3,)), dma, dma, dma((2,)), dma((2,)), dma((2,)), dma((2,)),
            dma((8,)), dma((8,)), dma((8,)), dma((8,)), dma((8,)), dma((8,)),
        ],
        compiler_params=pltpu.CompilerParams(
            collective_id=0, has_side_effects=True, vmem_limit_bytes=63 * 1024 * 1024
        ),
    )(fields, block_owner.reshape(1, count), ice_covered.reshape(1, count), land_mask)


def solution(mesh):
    placed = (
        P("comp", None, ("lat", "lon"), None),
        P(("lat", "lon")),
        P(("lat", "lon")),
        P(("lat", "lon"), None),
    )
    n_lat, n_lon = mesh.shape["lat"], mesh.shape["lon"]

    def body(fields, block_owner, ice_covered, land_mask):
        count = block_owner.shape[0]
        whole_tiles = count % (n_lat * n_lon * TILE) == 0 and count == BX
        if whole_tiles and n_lon > 2:
            return per_device_kernel(n_lat, n_lon, fields, block_owner, ice_covered, land_mask)
        return per_device(fields, block_owner, ice_covered, land_mask)

    return jax.shard_map(
        body,
        mesh=mesh,
        in_specs=placed,
        out_specs=P("comp", None, ("lat", "lon"), None),
        check_vma=False,
    )
```

profile of v0, /device:TPU:0, one launch (start us, length us, event | category | flops | bytes accessed | tf_op | source)
XLA Modules:
  0.0 34.4 jit_solution(9771778484327474138)
XLA Ops:
  0.0 33.7 %shard_map.46 = f32[1,2,128,256]{3,2,1,0:T(8,128)S(1)} custom-call(f32[1,7,128,256]{3,2,1,0:T(8,128)} %fields.1, s32[1,128]{1,0:T(1,128)} %bitcast.2, s32[1,128]{1,0:T(1,128)} %bitcast.3, s32[128,256]{1,0:T(8,128)} %land.1), custom_call_target="tpu_custom_call" | custom-call | tf_op jit(solution)/shard_map/pallas_call | solution.py:642
  33.7 0.7 %copy.6 = f32[1,2,128,256]{3,2,1,0:T(8,128)} copy(f32[1,2,128,256]{3,2,1,0:T(8,128)S(1)} %shard_map.46) | data formatting | bytes 524288
where the time goes:
time: 34.6 us; the launch traced here: 34.4 us
  Pallas kernels  33.7 us (97%)
  local copies, waits for them, and re-layouts  0.71 us (2%)
    pallas_call x1, Pallas kernels, per_device_kernel(): pl.pallas_call(functools.partial(step_kernel, n_lat, n_lon), out_shape=pl...  33.7 us
    unnamed x1, local copies, waits for them, and re-layouts  0.71 us

commit v1 on v0

v1 whole, which is shorter than its diff:
```python
import functools

import jax
import jax.numpy as jnp
from jax import lax
from jax.experimental import pallas as pl
from jax.experimental.pallas import tpu as pltpu
from jax.sharding import PartitionSpec as P

GX = 1
BY = 2
BX = 128
NSUB = 4


CD_ICE = 0.1
CW = 1.5
CSTAR = 2.0
ECC2 = 4.0
DMIN2 = 0.25
RELAX = 0.5
DTE = 0.5
CORIO = 0.3
MASS_FLOOR = 0.5
DRAG_FLOOR = 0.1


def from_behind(x, axis, by):
    size = lax.axis_size(axis)
    pairs = [(i, i + by) for i in range(size) if 0 <= i + by < size]
    return lax.ppermute(x, axis, pairs)


def with_halo(x, sides, width, wrap):
    for axis, dim in sides:
        size, length = (lax.axis_size(axis), x.shape[dim])
        up = [(i, (i + 1) % size) for i in range(size if wrap else size - 1)]
        down = [(j, i) for i, j in up]
        last = lax.slice_in_dim(x, length - width, length, axis=dim)
        first = lax.slice_in_dim(x, 0, width, axis=dim)
        before = lax.ppermute(last, axis, up)
        after = lax.ppermute(first, axis, down)
        x = jnp.concatenate([before, x, after], axis=dim)
    return x


def air_stress(ocean):
    wind_x, wind_y, current_x, current_y, tilt_x, tilt_y, density = ocean
    speed_ice = jnp.sqrt(wind_x * wind_x + wind_y * wind_y + 1.0)
    scale_ice = density * CD_ICE * speed_ice
    rel_x = wind_x - current_x
    rel_y = wind_y - current_y
    speed_open = jnp.sqrt(rel_x * rel_x + rel_y * rel_y + 1.0)
    scale_open = density * (0.1 + 0.05 * speed_open) * speed_open
    outbound = jnp.stack(
        [scale_ice * wind_x, scale_ice * wind_y, current_x, current_y, tilt_x, tilt_y]
    )
    open_stress = jnp.stack([scale_open * rel_x, scale_open * rel_y])
    return (outbound, open_stress)


def prepare(ice_tile, forcing, active):
    ice_mass = ice_tile[2]
    concentration = ice_tile[3]
    strength = ice_mass * jnp.exp(CSTAR * (concentration - 1.0)) * active
    drag_base = CW * concentration * active
    push_x = active * (concentration * forcing[0] - ice_mass * forcing[4])
    push_y = active * (concentration * forcing[1] - ice_mass * forcing[5])
    return jnp.stack(
        [strength, ice_mass, drag_base, push_x, push_y, forcing[2], forcing[3], active]
    )


def subcycle(ice_state, statics):
    east_vel, north_vel, stress_one, stress_two, stress_three = ice_state
    strength = statics[0]
    east_base = east_vel[:-1, :-1]
    north_base = north_vel[:-1, :-1]
    strain_xx = east_vel[:-1, 1:] - east_base
    strain_yy = north_vel[1:, :-1] - north_base
    shear = east_vel[1:, :-1] - east_base + (north_vel[:-1, 1:] - north_base)
    divergence = strain_xx + strain_yy
    tension = strain_xx - strain_yy
    delta_norm = jnp.sqrt(
        divergence * divergence + (tension * tension + shear * shear) / ECC2 + DMIN2
    )
    viscosity = strength[:-1, :-1] / delta_norm
    stress_sum = (stress_one[:-1, :-1] + RELAX * viscosity * (divergence - delta_norm)) / (
        1.0 + RELAX
    )
    stress_diff = (stress_two[:-1, :-1] + RELAX * viscosity * tension / ECC2) / (1.0 + RELAX)
    stress_shear = (stress_three[:-1, :-1] + RELAX * viscosity * shear / (2.0 * ECC2)) / (
        1.0 + RELAX
    )
    stress_xx = 0.5 * (stress_sum + stress_diff)
    stress_yy = 0.5 * (stress_sum - stress_diff)
    force_x = (
        stress_xx[1:, 1:] - stress_xx[1:, :-1] + (stress_shear[1:, 1:] - stress_shear[:-1, 1:])
    )
    force_y = (
        stress_shear[1:, 1:] - stress_shear[1:, :-1] + (stress_yy[1:, 1:] - stress_yy[:-1, 1:])
    )
    trimmed = statics[:, 1:-1, 1:-1]
    strength, ice_mass, drag_base, push_x, push_y, current_x, current_y, active = trimmed
    east_old = east_vel[1:-1, 1:-1]
    north_old = north_vel[1:-1, 1:-1]
    diff_x = current_x - east_old
    diff_y = current_y - north_old
    drag_coef = drag_base * jnp.sqrt(diff_x * diff_x + diff_y * diff_y + DRAG_FLOOR)
    denominator = jnp.maximum(ice_mass, MASS_FLOOR) / DTE + drag_coef
    east_new = (
        active
        * (
            ice_mass / DTE * east_old
            + force_x
            + push_x
            + drag_coef * current_x
            + CORIO * ice_mass * north_old
        )
        / denominator
    )
    north_new = (
        active
        * (
            ice_mass / DTE * north_old
            + force_y
            + push_y
            + drag_coef * current_y
            - CORIO * ice_mass * east_old
        )
        / denominator
    )
    new_state = jnp.stack(
        [east_new, north_new, stress_sum[1:, 1:], stress_diff[1:, 1:], stress_shear[1:, 1:]]
    )
    return (new_state, trimmed)


def give_back(ice_state, statics):
    east_vel = ice_state[0]
    north_vel = ice_state[1]
    drag_base = statics[2]
    current_x = statics[5]
    current_y = statics[6]
    diff_x = east_vel - current_x
    diff_y = north_vel - current_y
    factor = drag_base * jnp.sqrt(diff_x * diff_x + diff_y * diff_y + DRAG_FLOOR)
    return jnp.stack([factor * diff_x, factor * diff_y, drag_base / CW])


def to_tile(blocks):
    channels, count, cells = blocks.shape
    arranged = blocks.reshape(channels, count // GX, GX, BY, BX).transpose(0, 1, 3, 2, 4)
    return arranged.reshape(channels, count // GX * BY, GX * BX)


def from_tile(values):
    channels, rows, columns = values.shape
    arranged = values.reshape(channels, rows // BY, BY, GX, BX).transpose(0, 1, 3, 2, 4)
    return arranged.reshape(channels, rows // BY * GX, BY * BX)


def per_device(fields, block_owner, ice_covered, land_mask):
    count = block_owner.shape[0]
    is_ocean = lax.axis_index("comp") == 0
    outbound, open_stress = air_stress(fields[0])
    owner_row = block_owner.reshape(1, count)
    crossed = from_behind(outbound, "comp", 1)
    received, anchor = (
        lax.all_to_all(crossed, ("lat", "lon"), split_axis=1, concat_axis=1, tiled=True),
        lax.all_to_all(owner_row, ("lat", "lon"), split_axis=1, concat_axis=1, tiled=True),
    )
    local_ids = anchor[0] % count
    position = jnp.zeros((count,), jnp.int32).at[local_ids].set(jnp.arange(count, dtype=jnp.int32))
    forcing = to_tile(received[:, position])
    ice_tile = to_tile(fields[0])
    covered = ice_covered.astype(jnp.float32)[:, None] * (1 - land_mask).astype(jnp.float32)
    active = to_tile(covered[None])[0]
    statics = prepare(ice_tile, forcing, active)
    ice_state = jnp.stack([ice_tile[0], ice_tile[1], ice_tile[4], ice_tile[5], ice_tile[6]])
    joined = jnp.concatenate([ice_state, statics], 0)
    joined = with_halo(joined, (("lon", 2),), NSUB, True)
    joined = with_halo(joined, (("lat", 1),), NSUB, False)
    ice_state = joined[:5]
    statics = joined[5:]
    for repeat in range(NSUB):
        ice_state, statics = subcycle(ice_state, statics)
    returned = from_tile(give_back(ice_state, statics))
    back_send = returned[:, local_ids]
    regrouped = lax.all_to_all(back_send, ("lat", "lon"), split_axis=1, concat_axis=1, tiled=True)
    received_back = from_behind(regrouped, "comp", -1)
    ocean_out = received_back[:2] + (1.0 - received_back[2]) * open_stress
    ice_out = from_tile(ice_state[:2])
    return jnp.where(is_ocean, ocean_out, ice_out)[None]


TILE = 8
GROUP = 8
MESH = pl.DeviceIdType.MESH
U, V, MASS, CONC, S1, S2, S12, ACTIVE, PUSH_X, PUSH_Y, CUR_X, CUR_Y, STRENGTH, DRAG = range(14)
SIDES = [(a, b) for b in (-1, 1) for a in (0, -1, 1)]
ALL_AROUND = [(-1, 0), (1, 0)] + SIDES
ROUNDS = ((U, 8), (CUR_X, 2), (PUSH_X, 2))
KEEP = 1.0 / (1.0 + RELAX)


def tile_loop(tiles, together, body):
    def step(k, carry):
        for j in range(together):
            body(k * together + j)
        return carry
    lax.fori_loop(0, tiles // together, step, 0)


def pieces(values, axis):
    parts = []
    rest = values
    for piece in range(3):
        part = rest.astype(jnp.bfloat16)
        if piece < 2:
            rest = rest - part.astype(jnp.float32)
        parts.append(part)
    return jnp.concatenate(parts, axis=axis)


def dot_rows(thrice, values):
    return lax.dot_general(
        thrice, pieces(values, 0), (((1,), (0,)), ((), ())), preferred_element_type=jnp.float32
    )


def dot_lanes(thrice, values):
    return lax.dot_general(
        thrice, pieces(values, 1), (((1,), (1,)), ((), ())), preferred_element_type=jnp.float32
    )


def new_stress(strength, s1, s2, s12, u, v, u_east, v_east, u_up, v_up):
    sxx = u_east - u
    syy = v_up - v
    shear = (u_up - u) + (v_east - v)
    div = sxx + syy
    ten = sxx - syy
    square = div * div + (ten * ten + shear * shear) * (1.0 / ECC2) + DMIN2
    inverse = lax.rsqrt(square)
    visc = strength * inverse
    s1 = s1 * KEEP + visc * (div - square * inverse)
    s2 = s2 * KEEP + visc * ten * (1.0 / ECC2)
    s12 = s12 * KEEP + visc * shear * (0.5 / ECC2)
    return s1, s2, s12


def new_velocity(get, u, v, force_x, force_y):
    mass, cx, cy = get(MASS), get(CUR_X), get(CUR_Y)
    dx, dy = cx - u, cy - v
    square = dx * dx + dy * dy + DRAG_FLOOR
    drag = get(DRAG) * (square * lax.rsqrt(square))
    gain = get(ACTIVE) / (jnp.maximum(mass, MASS_FLOOR) * (1.0 / DTE) + drag)
    inertia = mass * (1.0 / DTE)
    turn = CORIO * mass
    return (
        gain * (inertia * u + force_x + get(PUSH_X) + drag * cx + turn * v),
        gain * (inertia * v + force_y + get(PUSH_Y) + drag * cy - turn * u),
    )


def step_kernel(
    n_lat, n_lon,
    fields, owner_hbm, covered_hbm, land, out,
    surf, open_st, ret, owner, covered, ids, recv, forc, one_hot, back, land_v,
    main, edge, flank, flank_back, flank_vel,
    rows_out0, rows_out1, rows_out2, rows_got0, rows_got1, rows_got2,
    side_out0, side_out1, side_out2, side_got0, side_got1, side_got2,
    load_sem, ids_ssem, ids_rsem, fwd_ssem, fwd_rsem, ret_ssem, ret_rsem, halo_ssem, halo_rsem,
):
    comp = lax.axis_index("comp")
    lat = lax.axis_index("lat")
    lon = lax.axis_index("lon")
    peers = n_lat * n_lon
    me = lat * n_lon + lon
    count = owner.shape[1]
    per = count // peers
    width = BX
    barrier = pltpu.get_barrier_semaphore()
    rows_out = (rows_out0, rows_out1, rows_out2)
    rows_got = (rows_got0, rows_got1, rows_got2)
    side_out = (side_out0, side_out1, side_out2)
    side_got = (side_got0, side_got1, side_got2)

    def rows_of(peer):
        return pl.ds(pl.multiple_of(peer * per, per), per)

    def device(kind, peer):
        return (kind, peer // n_lon, peer % n_lon)

    def each_peer(body):
        def step(k, carry):
            body((me + k) % peers)
            return carry
        lax.fori_loop(0, peers, step, 0)

    def signal_peers(kind):
        each_peer(
            lambda p: pl.semaphore_signal(
                barrier, inc=1, device_id=device(kind, p), device_id_type=MESH
            )
        )

    def send_rows(kind, src, lo, num, dst, dlo, ssem, rsem):
        def body(p):
            pltpu.make_async_remote_copy(
                src_ref=src.at[pl.ds(lo, num), rows_of(p), :],
                dst_ref=dst.at[pl.ds(dlo, num), rows_of(me), :],
                send_sem=ssem, recv_sem=rsem,
                device_id=device(kind, p), device_id_type=MESH,
            ).start()
        each_peer(body)

    def wait_bytes(ref, sem):
        pltpu.make_async_copy(ref, ref, sem).wait()

    @pl.when(comp == 0)
    def _ocean():
        signal_peers(1)
        names = pltpu.make_async_copy(owner_hbm, owner, load_sem.at[3])
        raw = pltpu.make_async_copy(fields.at[0, pl.ds(2, 4)], surf.at[pl.ds(2, 4)], load_sem.at[0])
        wind = pltpu.make_async_copy(fields.at[0, pl.ds(0, 2)], surf.at[pl.ds(0, 2)], load_sem.at[1])
        rho = pltpu.make_async_copy(fields.at[0, pl.ds(6, 1)], surf.at[pl.ds(6, 1)], load_sem.at[2])
        names.start()
        raw.start()
        wind.start()
        rho.start()
        names.wait()
        with jax.named_scope("o_barrier"):
            pl.semaphore_wait(barrier, peers)

        def ids_out(p):
            pltpu.make_async_remote_copy(
                src_ref=owner, dst_ref=ids.at[me], send_sem=ids_ssem, recv_sem=ids_rsem,
                device_id=device(1, p), device_id_type=MESH,
            ).start()
        with jax.named_scope("o_send4"):
            each_peer(ids_out)
            raw.wait()
            send_rows(1, surf, 2, 4, recv, 2, fwd_ssem.at[0], fwd_rsem.at[0])
            wind.wait()
            rho.wait()

        def stress(t):
            r = pl.ds(pl.multiple_of(t * TILE, TILE), TILE)
            wx, wy, density = surf[0, r, :], surf[1, r, :], surf[6, r, :]
            scale = density * CD_ICE * jnp.sqrt(wx * wx + wy * wy + 1.0)
            forc[0, r, :] = scale * wx
            forc[1, r, :] = scale * wy

        with jax.named_scope("o_stress"):
            tile_loop(count // TILE, 2, stress)
            send_rows(1, forc, 0, 2, recv, 0, fwd_ssem.at[1], fwd_rsem.at[1])

        def open_water(t):
            r = pl.ds(pl.multiple_of(t * TILE, TILE), TILE)
            density = surf[6, r, :]
            rel_x = surf[0, r, :] - surf[2, r, :]
            rel_y = surf[1, r, :] - surf[3, r, :]
            speed = jnp.sqrt(rel_x * rel_x + rel_y * rel_y + 1.0)
            scale = density * (0.1 + 0.05 * speed) * speed
            open_st[0, r, :] = scale * rel_x
            open_st[1, r, :] = scale * rel_y

        tile_loop(count // TILE, 2, open_water)
        with jax.named_scope("o_waitret1"):
            wait_bytes(ret.at[pl.ds(2, 1)], ret_rsem.at[0])
        with jax.named_scope("o_waitret2"):
            wait_bytes(ret.at[pl.ds(0, 2)], ret_rsem.at[1])

        def finish(t):
            r = pl.ds(pl.multiple_of(t * TILE, TILE), TILE)
            water = 1.0 - ret[2, r, :]
            out[0, 0, r, :] = ret[0, r, :] + water * open_st[0, r, :]
            out[0, 1, r, :] = ret[1, r, :] + water * open_st[1, r, :]

        with jax.named_scope("o_finish"):
            tile_loop(count // TILE, 2, finish)
        wait_bytes(ids, ids_ssem)
        wait_bytes(surf.at[pl.ds(2, 4)], fwd_ssem.at[0])
        wait_bytes(forc.at[pl.ds(0, 2)], fwd_ssem.at[1])

    @pl.when(comp == 1)
    def _ice():
        def inside(a):
            if a == 0:
                return lat >= 0
            return lat + a >= 0 if a < 0 else lat + a < n_lat

        def around(a, b):
            return (1, lat + a, (lon + b + n_lon) % n_lon)

        signal_peers(0)
        for a, b in ALL_AROUND:
            @pl.when(inside(a))
            def _():
                pl.semaphore_signal(barrier, inc=1, device_id=around(a, b), device_id_type=MESH)
        loads = [
            pltpu.make_async_copy(
                fields.at[0, :, :, pl.ds(y * width, width)], main.at[pl.ds(0, 7), y], load_sem.at[y]
            )
            for y in range(2)
        ]
        loads.append(pltpu.make_async_copy(land, land_v, load_sem.at[2]))
        loads.append(pltpu.make_async_copy(covered_hbm, covered, load_sem.at[3]))
        for load in loads:
            load.start()

        tiles = count // TILE
        top, bottom = pl.ds(0, TILE), pl.ds(count - TILE, TILE)
        zero_tile = jnp.zeros((TILE, width), jnp.float32)
        for wall, which in ((lat == 0, 0), (lat == n_lat - 1, 1)):
            @pl.when(wall)
            def _():
                for e in range(3):
                    for k in range(rows_got[e].shape[1]):
                        rows_got[e][which, k] = zero_tile
                    for k in range(2):
                        side_got[e][2 * which, k] = zero_tile

        def clear(t):
            r = pl.ds(pl.multiple_of(t * TILE, TILE), TILE)
            for c in range(2):
                for y in range(2):
                    flank_back[c, y, r, :] = zero_tile
                    flank_vel[c, y, r, :] = zero_tile

        tile_loop(tiles, 2, clear)
        for load in loads:
            load.wait()
        diag = lax.broadcasted_iota(jnp.int32, (count, count), 0) == lax.broadcasted_iota(
            jnp.int32, (count, count), 1
        )
        wet = jnp.sum(
            jnp.where(diag, covered[...].astype(jnp.float32), 0.0), axis=1, keepdims=True
        )
        sea = wet * (1 - land_v[...]).astype(jnp.float32)
        for y in range(2):
            main[ACTIVE, y] = sea[:, y * width:(y + 1) * width]

        lane = lax.broadcasted_iota(jnp.int32, (TILE, width), 1)
        sub = lax.broadcasted_iota(jnp.int32, (TILE, width), 0)
        pick_row = lax.broadcasted_iota(jnp.int32, (2 * TILE, width), 0)
        pick_col = lax.broadcasted_iota(jnp.int32, (2 * TILE, width), 1)
        picked = jnp.where(pick_row < TILE, pick_row, pick_row + (width - 2 * TILE)) == pick_col
        picker = jnp.where(picked, 1.0, 0.0).astype(jnp.bfloat16)
        picker = jnp.concatenate([picker] * 3, axis=1)

        def pack(e):
            lo, num = ROUNDS[e]
            west, east = zero_tile, zero_tile
            for k in range(num // 2):
                ups, downs = zero_tile, zero_tile
                for i in range(4):
                    c, y = lo + 2 * k + i // 2, i % 2
                    head, foot = main[c, y, top, :], main[c, y, bottom, :]
                    here = (sub >= 2 * i) & (sub < 2 * i + 2)
                    ups = jnp.where(here, pltpu.roll(head, 2 * i, 0) if i else head, ups)
                    downs = jnp.where(here, pltpu.roll(foot, (2 * i + 2) % TILE, 0) if i < 3 else foot, downs)
                    ends = jnp.where(sub < NSUB, head, foot)
                    slot = (k * 4 + i) * NSUB
                    mine = (lane >= slot) & (lane < slot + NSUB)
                    west = jnp.where(mine, pltpu.roll(ends, slot, 1) if slot else ends, west)
                    east = jnp.where(mine, pltpu.roll(ends, (slot + NSUB) % width, 1), east)
                rows_out[e][0, k] = ups
                rows_out[e][1, k] = downs
            side_out[e][0] = west
            side_out[e][1] = east
            for c in range(lo, lo + num):
                for y in range(2):
                    across = dot_lanes(picker, main[c, y])
                    flank[c, y, pl.ds(TILE, TILE), :] = across[:TILE]
                    flank[c, y, pl.ds(2 * TILE, TILE), :] = across[TILE:]

        def halo(e, begin):
            lo, num = ROUNDS[e]
            moves = []
            for a in (-1, 1):
                k = 1 if a > 0 else 0
                moves.append((a, 0, rows_out[e].at[k], rows_got[e].at[1 - k]))
            for a, b in SIDES:
                k = 1 if b > 0 else 0
                moves.append((a, b, side_out[e].at[k], side_got[e].at[1 - a, 1 - k]))
            for b in (-1, 1):
                src, dst = (2 * TILE, 0) if b > 0 else (TILE, 3 * TILE)
                moves.append((
                    0, b,
                    flank.at[pl.ds(lo, num), :, pl.ds(src, TILE), :],
                    flank.at[pl.ds(lo, num), :, pl.ds(dst, TILE), :],
                ))
            for k, (a, b, src, dst) in enumerate(moves):
                copy = pltpu.make_async_remote_copy(
                    src_ref=src, dst_ref=dst,
                    send_sem=halo_ssem.at[e, k], recv_sem=halo_rsem.at[e, k],
                    device_id=around(a, b), device_id_type=MESH,
                )
                if begin:
                    @pl.when(inside(a))
                    def _():
                        copy.start()
                else:
                    @pl.when(inside(a))
                    def _():
                        copy.wait_send()

                    @pl.when(inside(-a))
                    def _():
                        copy.wait_recv()

        def unpack(e):
            lo, num = ROUNDS[e]
            got, side = rows_got[e], side_got[e]
            ends = []
            for k in range(2):
                far, near = side[0, k], side[1, k]
                ends.append(pltpu.roll(jnp.where(sub >= TILE - 2, far, near), 2, 0))
            for k in range(2):
                far, near = side[2, k], side[1, k]
                ends.append(pltpu.roll(jnp.where(sub < 2, far, near), TILE - 2, 0))
            for k in range(num // 2):
                for i in range(4):
                    c, y = lo + 2 * k + i // 2, i % 2
                    slot = (k * 4 + i) * NSUB
                    for strip in range(2):
                        own = main[c, y, top if strip == 0 else bottom, :]
                        beyond = got[strip, k]
                        if strip == 0:
                            beyond = pltpu.roll(beyond, (TILE - 2 * i) % TILE, 0) if i else beyond
                            body = jnp.where(sub < 2, beyond, pltpu.roll(own, 2, 0))
                        else:
                            beyond = pltpu.roll(beyond, TILE - 2 - 2 * i, 0) if i < 3 else beyond
                            body = jnp.where(sub >= TILE - 2, beyond, pltpu.roll(own, TILE - 2, 0))
                        from_west, from_east = ends[2 * strip], ends[2 * strip + 1]
                        from_east = pltpu.roll(from_east, width - slot, 1) if slot else from_east
                        from_west = pltpu.roll(from_west, width - NSUB - slot, 1)
                        edge[c, strip, y, :, pl.ds(0, width)] = body
                        edge[c, strip, y, :, pl.ds(width, width)] = jnp.where(
                            lane < NSUB, from_east, jnp.where(lane >= width - NSUB, from_west, 0.0)
                        )

        def derive(load, store):
            conc, act = load(CONC), load(ACTIVE)
            store(STRENGTH, (RELAX * KEEP) * load(MASS) * jnp.exp(CSTAR * (conc - 1.0)) * act)
            store(DRAG, CW * conc * act)

        def derive_main(t):
            r = pl.ds(pl.multiple_of(t * TILE, TILE), TILE)
            for y in range(2):
                def store(c, x):
                    main[c, y, r, :] = x
                derive(lambda c: main[c, y, r, :], store)

        def derive_edges():
            for y in range(2):
                for strip in range(2):
                    def store(c, x):
                        edge[c, strip, y] = x
                    derive(lambda c: edge[c, strip, y], store)

                def store(c, x):
                    flank[c, y] = x
                derive(lambda c: flank[c, y], store)

        def sweep_main(g, stress, velocity):
            spots = [
                pl.ds(pl.multiple_of((g * GROUP + j) * TILE, TILE), TILE) for j in range(GROUP)
            ]
            behind = pl.ds(pl.multiple_of(jnp.maximum(g * GROUP - 1, 0) * TILE, TILE), TILE)
            ahead = pl.ds(
                pl.multiple_of(jnp.minimum(g * GROUP + GROUP, tiles - 1) * TILE, TILE), TILE
            )
            vels = [[(main[U, y, r, :], main[V, y, r, :]) for y in range(2)] for r in spots]
            stresses = []
            if stress:
                follow = (main[U, 0, ahead, :], main[V, 0, ahead, :])
            for j, r in enumerate(spots):
                old = [tuple(main[c, y, r, :] for c in (S1, S2, S12)) for y in range(2)]
                if not stress:
                    stresses.append(old)
                    continue
                beyond = vels[j + 1][0] if j + 1 < GROUP else follow
                row = []
                for y in range(2):
                    u, v = vels[j][y]
                    if y == 0:
                        u_up, v_up = vels[j][1]
                    else:
                        u_up, v_up = (
                            pltpu.roll(jnp.where(sub == 0, after, x), TILE - 1, 0)
                            for x, after in zip(vels[j][0], beyond)
                        )
                    fresh = new_stress(
                        main[STRENGTH, y, r, :], *old[y], u, v,
                        pltpu.roll(u, width - 1, 1), pltpu.roll(v, width - 1, 1), u_up, v_up,
                    )
                    for c, x in zip((S1, S2, S12), fresh):
                        main[c, y, r, :] = x
                    row.append(fresh)
                stresses.append(row)
            if not velocity:
                return
            yy_before = 0.5 * (main[S1, 1, behind, :] - main[S2, 1, behind, :])
            cross_before = main[S12, 1, behind, :]
            for j, r in enumerate(spots):
                xx = [0.5 * (s1 + s2) for s1, s2, _ in stresses[j]]
                yy = [0.5 * (s1 - s2) for s1, s2, _ in stresses[j]]
                cross = [s12 for _, _, s12 in stresses[j]]
                yy_down, cross_down = (
                    [pltpu.roll(jnp.where(sub == TILE - 1, before, x[1]), 1, 0), x[0]]
                    for x, before in ((yy, yy_before), (cross, cross_before))
                )
                yy_before, cross_before = yy[1], cross[1]
                for y in range(2):
                    force_x = xx[y] - pltpu.roll(xx[y], 1, 1) + (cross[y] - cross_down[y])
                    force_y = cross[y] - pltpu.roll(cross[y], 1, 1) + (yy[y] - yy_down[y])
                    u, v = new_velocity(lambda c: main[c, y, r, :], *vels[j][y], force_x, force_y)
                    main[U, y, r, :] = u
                    main[V, y, r, :] = v

        def sweep_edge(stress, velocity):
            for strip in range(2):
                vels = [(edge[U, strip, y], edge[V, strip, y]) for y in range(2)]
                fresh = [tuple(edge[c, strip, y] for c in (S1, S2, S12)) for y in range(2)]
                if stress:
                    ups = [vels[1], tuple(pltpu.roll(x, TILE - 1, 0) for x in vels[0])]
                    for y in range(2):
                        east = [pltpu.roll(x, 2 * width - 1, 1) for x in vels[y]]
                        fresh[y] = new_stress(
                            edge[STRENGTH, strip, y], *fresh[y], *vels[y], *east, *ups[y]
                        )
                        for c, x in zip((S1, S2, S12), fresh[y]):
                            edge[c, strip, y] = x
                if not velocity:
                    continue
                xx = [0.5 * (s1 + s2) for s1, s2, _ in fresh]
                yy = [0.5 * (s1 - s2) for s1, s2, _ in fresh]
                cross = [s12 for _, _, s12 in fresh]
                yy_down, cross_down = ([pltpu.roll(x[1], 1, 0), x[0]] for x in (yy, cross))
                for y in range(2):
                    force_x = xx[y] - pltpu.roll(xx[y], 1, 1) + (cross[y] - cross_down[y])
                    force_y = cross[y] - pltpu.roll(cross[y], 1, 1) + (yy[y] - yy_down[y])
                    u, v = new_velocity(lambda c: edge[c, strip, y], *vels[y], force_x, force_y)
                    edge[U, strip, y] = u
                    edge[V, strip, y] = v

        def sweep_flank(stress, velocity):
            spots = [pl.ds(j * TILE, TILE) for j in range(4)]
            vels = [[(flank[U, y, r, :], flank[V, y, r, :]) for y in range(2)] for r in spots]
            fresh = [
                [tuple(flank[c, y, r, :] for c in (S1, S2, S12)) for y in range(2)] for r in spots
            ]
            if stress:
                for j, r in enumerate(spots):
                    for y in range(2):
                        after = vels[min(j + 1, 3)][y]
                        east = [
                            pltpu.roll(jnp.where(sub == 0, b, x), TILE - 1, 0)
                            for x, b in zip(vels[j][y], after)
                        ]
                        ups = vels[j][1] if y == 0 else [
                            pltpu.roll(x, width - 1, 1) for x in vels[j][0]
                        ]
                        fresh[j][y] = new_stress(
                            flank[STRENGTH, y, r, :], *fresh[j][y], *vels[j][y], *east, *ups
                        )
                        for c, x in zip((S1, S2, S12), fresh[j][y]):
                            flank[c, y, r, :] = x
            if not velocity:
                return
            xx = [[0.5 * (s1 + s2) for s1, s2, _ in row] for row in fresh]
            yy = [[0.5 * (s1 - s2) for s1, s2, _ in row] for row in fresh]
            cross = [[s12 for _, _, s12 in row] for row in fresh]

            def westward(x, j, y):
                before = x[max(j - 1, 0)][y]
                return pltpu.roll(jnp.where(sub == TILE - 1, before, x[j][y]), 1, 0)

            def downward(x, j, y):
                return x[j][0] if y == 1 else pltpu.roll(x[j][1], 1, 1)

            for j, r in enumerate(spots):
                for y in range(2):
                    force_x = xx[j][y] - westward(xx, j, y) + (cross[j][y] - downward(cross, j, y))
                    force_y = cross[j][y] - westward(cross, j, y) + (yy[j][y] - downward(yy, j, y))
                    u, v = new_velocity(lambda c: flank[c, y, r, :], *vels[j][y], force_x, force_y)
                    flank[U, y, r, :] = u
                    flank[V, y, r, :] = v

        walls = jnp.where(lat == 0, 3, 0) + jnp.where(lat == n_lat - 1, 3, 0)
        with jax.named_scope("i_barrier"):
            pl.semaphore_wait(barrier, peers + 8 - walls)
        with jax.named_scope("i_pack0"):
            pack(0)
            halo(0, True)
        tile_loop(tiles, 2, derive_main)

        with jax.named_scope("i_waitids"):
            wait_bytes(ids, ids_rsem)
        wanted = me * per
        row_lane = lax.broadcasted_iota(jnp.int32, (per, count), 1)
        row_sub = lax.broadcasted_iota(jnp.int32, (per, count), 0)
        mine = row_lane == row_sub + wanted
        blocks = lax.broadcasted_iota(jnp.int32, (per, count), 1).astype(jnp.float32)
        base = (me * count).astype(jnp.float32)
        for p in range(peers):
            owned = jnp.broadcast_to(ids[p], (per, count)).astype(jnp.float32)
            local = jnp.sum(jnp.where(mine, owned, 0.0), axis=1, keepdims=True) - base
            one_hot[pl.ds(p * per, per), :] = jnp.where(local == blocks, 1.0, 0.0)

        with jax.named_scope("i_waithalo0"):
            halo(0, False)
        with jax.named_scope("i_unpack0"):
            unpack(0)
            derive_edges()
        groups = tiles // GROUP
        with jax.named_scope("i_stress"):
            tile_loop(groups, 1, lambda g: sweep_main(g, True, False))
            sweep_edge(True, False)
            sweep_flank(True, False)
        by_slot = one_hot[...]
        to_slots = jnp.concatenate([by_slot.astype(jnp.bfloat16)] * 3, axis=1)
        to_blocks = jnp.concatenate([by_slot.T.astype(jnp.bfloat16)] * 3, axis=1)

        with jax.named_scope("i_waitf4"):
            wait_bytes(recv.at[pl.ds(2, 4)], fwd_rsem.at[0])
        for c in range(2):
            both = dot_rows(to_blocks, recv[2 + c])
            for y in range(2):
                main[CUR_X + c, y] = both[:, y * width:(y + 1) * width]
        with jax.named_scope("i_packmid"):
            pack(1)
            halo(1, True)
        for c in range(2):
            both = dot_rows(to_blocks, recv[4 + c])
            for y in range(2):
                main[PUSH_X + c, y] = main[MASS, y] * both[:, y * width:(y + 1) * width]
        for y in range(2):
            share = main[CONC, y] * main[ACTIVE, y]
            back[2, :, pl.ds(y * width, width)] = dot_rows(to_slots, share)
        send_rows(0, back, 2, 1, ret, 2, ret_ssem.at[0], ret_rsem.at[0])

        with jax.named_scope("i_waitf2"):
            wait_bytes(recv.at[pl.ds(0, 2)], fwd_rsem.at[1])
        with jax.named_scope("i_push"):
            for c in range(2):
                both = dot_rows(to_blocks, recv[c])
                for y in range(2):
                    main[PUSH_X + c, y] = main[ACTIVE, y] * (
                        main[CONC, y] * both[:, y * width:(y + 1) * width] - main[PUSH_X + c, y]
                    )
        with jax.named_scope("i_packlate"):
            pack(2)
            halo(2, True)

        with jax.named_scope("i_vel1"):
            tile_loop(groups, 1, lambda g: sweep_main(g, False, True))
        with jax.named_scope("i_sweeps"):
            tile_loop((NSUB - 1) * groups, 1, lambda k: sweep_main(k % groups, True, True))
        with jax.named_scope("i_waitmid"):
            halo(1, False)
        unpack(1)
        with jax.named_scope("i_waitlate"):
            halo(2, False)
        with jax.named_scope("i_edge"):
            unpack(2)
            sweep_edge(False, True)
            tile_loop(NSUB - 1, 1, lambda k: sweep_edge(True, True))
        with jax.named_scope("i_flank"):
            sweep_flank(False, True)
            tile_loop(NSUB - 1, 1, lambda k: sweep_flank(True, True))

        def leave(get, u, v):
            dx, dy = u - get(CUR_X), v - get(CUR_Y)
            drag = get(DRAG) * jnp.sqrt(dx * dx + dy * dy + DRAG_FLOOR)
            return drag * dx, drag * dy

        outer = (lane < NSUB) | (lane >= width - NSUB)

        with jax.named_scope("i_returned"):
            for y in range(2):
                for c in (U, V):
                    north = pltpu.roll(edge[c, 0, y, :, pl.ds(0, width)], TILE - 2, 0)
                    south = pltpu.roll(edge[c, 1, y, :, pl.ds(0, width)], 2, 0)
                    main[c, y, top, :] = jnp.where(sub < 2, north, main[c, y, top, :])
                    main[c, y, bottom, :] = jnp.where(sub >= TILE - 2, south, main[c, y, bottom, :])
                for j, far in ((1, 0), (2, count - TILE)):
                    r = pl.ds(j * TILE, TILE)
                    held = (lane >= 2) & (lane < count - 2)
                    held = held & ((sub < NSUB) if j == 1 else (sub >= TILE - NSUB))
                    u, v = flank[U, y, r, :], flank[V, y, r, :]
                    gone = leave(lambda c: flank[c, y, r, :], u, v)
                    for c in range(2):
                        flank_back[c, y, pl.ds(far, TILE), :] = jnp.where(held, gone[c], 0.0)
                        flank_vel[c, y, pl.ds(far, TILE), :] = jnp.where(held, (u, v)[c], 0.0)

            def returned(t):
                r = pl.ds(pl.multiple_of(t * TILE, TILE), TILE)
                block = sub + t * TILE
                theirs = outer & (block >= 2) & (block < count - 2)
                for y in range(2):
                    half = pl.ds(y * width, width)
                    u, v = main[U, y, r, :], main[V, y, r, :]
                    gone = leave(lambda c: main[c, y, r, :], u, v)
                    for c in range(2):
                        forc[c, r, half] = jnp.where(theirs, 0.0, gone[c])
                        out[0, c, r, half] = jnp.where(theirs, 0.0, (u, v)[c])

            tile_loop(tiles, 2, returned)
        with jax.named_scope("i_back"):
            for c in range(2):
                both = dot_rows(to_slots, forc[c])
                for y in range(2):
                    part = both[:, y * width:(y + 1) * width]
                    back[c, :, pl.ds(y * width, width)] = part + dot_lanes(to_slots, flank_back[c, y])
            send_rows(0, back, 0, 2, ret, 0, ret_ssem.at[1], ret_rsem.at[1])
        same = jnp.where(diag, 1.0, 0.0).astype(jnp.bfloat16)
        same = jnp.concatenate([same] * 3, axis=1)
        for c in range(2):
            for y in range(2):
                half = pl.ds(y * width, width)
                out[0, c, :, half] += dot_lanes(same, flank_vel[c, y])
        wait_bytes(back.at[pl.ds(2, 1)], ret_ssem.at[0])
        wait_bytes(back.at[pl.ds(0, 2)], ret_ssem.at[1])


def per_device_kernel(n_lat, n_lon, fields, block_owner, ice_covered, land_mask):
    count, cells = land_mask.shape
    peers = n_lat * n_lon
    f32 = jnp.float32
    anywhere = pl.BlockSpec(memory_space=pl.ANY)
    in_vmem = pl.BlockSpec(memory_space=pltpu.VMEM)
    dma = pltpu.SemaphoreType.DMA
    halos = [pltpu.VMEM((2, num // 2, TILE, BX), f32) for _, num in ROUNDS] * 2
    sides = [pltpu.VMEM((2, TILE, BX), f32) for _ in ROUNDS]
    sides += [pltpu.VMEM((3, 2, TILE, BX), f32) for _ in ROUNDS]
    return pl.pallas_call(
        functools.partial(step_kernel, n_lat, n_lon),
        out_shape=pltpu.VMEM((1, 2, count, cells), f32),
        in_specs=[anywhere, anywhere, anywhere, anywhere],
        out_specs=in_vmem,
        scratch_shapes=[
            pltpu.VMEM((7, count, cells), f32),
            pltpu.VMEM((2, count, cells), f32),
            pltpu.VMEM((3, count, cells), f32),
            pltpu.VMEM((1, count), jnp.int32),
            pltpu.VMEM((1, count), jnp.int32),
            pltpu.VMEM((peers, 1, count), jnp.int32),
            pltpu.VMEM((6, count, cells), f32),
            pltpu.VMEM((2, count, cells), f32),
            pltpu.VMEM((count, count), f32),
            pltpu.VMEM((3, count, cells), f32),
            pltpu.VMEM((count, cells), jnp.int32),
            pltpu.VMEM((14, 2, count, BX), f32),
            pltpu.VMEM((14, 2, 2, TILE, 2 * BX), f32),
            pltpu.VMEM((14, 2, 4 * TILE, BX), f32),
            pltpu.VMEM((2, 2, BX, count), f32),
            pltpu.VMEM((2, 2, BX, count), f32),
            *halos, *sides,
            dma((4,)), dma, dma, dma((2,)), dma((2,)), dma((2,)), dma((2,)),
            dma((3, 10)), dma((3, 10)),
        ],
        compiler_params=pltpu.CompilerParams(
            collective_id=0, has_side_effects=True, vmem_limit_bytes=63 * 1024 * 1024
        ),
    )(fields, block_owner.reshape(1, count), ice_covered.reshape(1, count), land_mask)


def solution(mesh):
    placed = (
        P("comp", None, ("lat", "lon"), None),
        P(("lat", "lon")),
        P(("lat", "lon")),
        P(("lat", "lon"), None),
    )
    n_lat, n_lon = mesh.shape["lat"], mesh.shape["lon"]

    def body(fields, block_owner, ice_covered, land_mask):
        count = block_owner.shape[0]
        whole_tiles = count % (n_lat * n_lon * TILE) == 0 and count == BX
        if whole_tiles and n_lon > 2:
            return per_device_kernel(n_lat, n_lon, fields, block_owner, ice_covered, land_mask)
        return per_device(fields, block_owner, ice_covered, land_mask)

    return jax.shard_map(
        body,
        mesh=mesh,
        in_specs=placed,
        out_specs=P("comp", None, ("lat", "lon"), None),
        check_vma=False,
    )
```

time: 34.6 us -> 30.1 us (0.87)
  Pallas kernels: 33.7 us -> 29.2 us
    pallas_call x1, Pallas kernels: 33.7 us -> 29.2 us  [per_device_kernel(): pl.pallas_call(functools.partial(step_kernel, n_lat, n_lon), out_shape=pl...]
where the time goes in v1:
time: 30.1 us; the launch traced here: 29.9 us
  Pallas kernels  29.2 us (97%)
  local copies, waits for them, and re-layouts  0.71 us (2%)
    pallas_call x1, Pallas kernels, per_device_kernel(): pl.pallas_call(functools.partial(step_kernel, n_lat, n_lon), out_shape=pl...  29.2 us
    unnamed x1, local copies, waits for them, and re-layouts  0.71 us

profile of v1, /device:TPU:0, one launch (start us, length us, event | category | flops | bytes accessed | tf_op | source)
XLA Modules:
  0.0 29.9 jit_solution(18387404271571691133)
XLA Ops:
  0.0 29.2 %shard_map.46 = f32[1,2,128,256]{3,2,1,0:T(8,128)S(1)} custom-call(f32[1,7,128,256]{3,2,1,0:T(8,128)} %fields.1, s32[1,128]{1,0:T(1,128)} %bitcast.2, s32[1,128]{1,0:T(1,128)} %bitcast.3, s32[128,256]{1,0:T(8,128)} %land.1), custom_call_target="tpu_custom_call" | custom-call | tf_op jit(solution)/shard_map/pallas_call | solution.py:841
  29.2 0.7 %copy.6 = f32[1,2,128,256]{3,2,1,0:T(8,128)} copy(f32[1,2,128,256]{3,2,1,0:T(8,128)S(1)} %shard_map.46) | data formatting | bytes 524288

commit v2 on v1

--- a/solution.py
+++ b/solution.py
@@ -266,8 +266,8 @@
 
 def step_kernel(
     n_lat, n_lon,
-    fields, owner_hbm, covered_hbm, land, out,
-    surf, open_st, ret, owner, covered, ids, recv, forc, one_hot, back, land_v,
+    fields, owner_hbm, covered_hbm, land, ret, here,
+    surf, stay, owner, covered, ids, recv, forc, one_hot, back, land_v,
     main, edge, flank, flank_back, flank_vel,
     rows_out0, rows_out1, rows_out2, rows_got0, rows_got1, rows_got2,
     side_out0, side_out1, side_out2, side_got0, side_got1, side_got2,
@@ -294,8 +294,10 @@
         return (kind, peer // n_lon, peer % n_lon)
 
     def each_peer(body):
+        beyond = jnp.where(lat < n_lat // 2, n_lat // 2, 0)
+
         def step(k, carry):
-            body((me + k) % peers)
+            body((beyond + k // n_lon) % n_lat * n_lon + (lon + k) % n_lon)
             return carry
         lax.fori_loop(0, peers, step, 0)
 
@@ -318,6 +320,11 @@
 
     def wait_bytes(ref, sem):
         pltpu.make_async_copy(ref, ref, sem).wait()
+
+    def keep_here():
+        copy = pltpu.make_async_copy(stay, here, load_sem.at[4])
+        copy.start()
+        copy.wait()
 
     @pl.when(comp == 0)
     def _ocean():
@@ -364,23 +371,16 @@
             rel_y = surf[1, r, :] - surf[3, r, :]
             speed = jnp.sqrt(rel_x * rel_x + rel_y * rel_y + 1.0)
             scale = density * (0.1 + 0.05 * speed) * speed
-            open_st[0, r, :] = scale * rel_x
-            open_st[1, r, :] = scale * rel_y
+            stay[0, r, :] = scale * rel_x
+            stay[1, r, :] = scale * rel_y
 
         tile_loop(count // TILE, 2, open_water)
+        keep_here()
         with jax.named_scope("o_waitret1"):
             wait_bytes(ret.at[pl.ds(2, 1)], ret_rsem.at[0])
         with jax.named_scope("o_waitret2"):
             wait_bytes(ret.at[pl.ds(0, 2)], ret_rsem.at[1])
 
-        def finish(t):
-            r = pl.ds(pl.multiple_of(t * TILE, TILE), TILE)
-            water = 1.0 - ret[2, r, :]
-            out[0, 0, r, :] = ret[0, r, :] + water * open_st[0, r, :]
-            out[0, 1, r, :] = ret[1, r, :] + water * open_st[1, r, :]
-
-        with jax.named_scope("o_finish"):
-            tile_loop(count // TILE, 2, finish)
         wait_bytes(ids, ids_ssem)
         wait_bytes(surf.at[pl.ds(2, 4)], fwd_ssem.at[0])
         wait_bytes(forc.at[pl.ds(0, 2)], fwd_ssem.at[1])
@@ -742,7 +742,6 @@
         for y in range(2):
             share = main[CONC, y] * main[ACTIVE, y]
             back[2, :, pl.ds(y * width, width)] = dot_rows(to_slots, share)
-        send_rows(0, back, 2, 1, ret, 2, ret_ssem.at[0], ret_rsem.at[0])
 
         with jax.named_scope("i_waitf2"):
             wait_bytes(recv.at[pl.ds(0, 2)], fwd_rsem.at[1])
@@ -761,18 +760,20 @@
             tile_loop(groups, 1, lambda g: sweep_main(g, False, True))
         with jax.named_scope("i_sweeps"):
             tile_loop((NSUB - 1) * groups, 1, lambda k: sweep_main(k % groups, True, True))
+        send_rows(0, back, 2, 1, ret, 2, ret_ssem.at[0], ret_rsem.at[0])
         with jax.named_scope("i_waitmid"):
             halo(1, False)
         unpack(1)
         with jax.named_scope("i_waitlate"):
             halo(2, False)
+        def sweep_strips(stress, velocity):
+            sweep_flank(stress, velocity)
+            sweep_edge(stress, velocity)
+
         with jax.named_scope("i_edge"):
             unpack(2)
-            sweep_edge(False, True)
-            tile_loop(NSUB - 1, 1, lambda k: sweep_edge(True, True))
-        with jax.named_scope("i_flank"):
-            sweep_flank(False, True)
-            tile_loop(NSUB - 1, 1, lambda k: sweep_flank(True, True))
+            sweep_strips(False, True)
+            tile_loop(NSUB - 1, 1, lambda k: sweep_strips(True, True))
 
         def leave(get, u, v):
             dx, dy = u - get(CUR_X), v - get(CUR_Y)
@@ -808,7 +809,7 @@
                     gone = leave(lambda c: main[c, y, r, :], u, v)
                     for c in range(2):
                         forc[c, r, half] = jnp.where(theirs, 0.0, gone[c])
-                        out[0, c, r, half] = jnp.where(theirs, 0.0, (u, v)[c])
+                        stay[c, r, half] = jnp.where(theirs, 0.0, (u, v)[c])
 
             tile_loop(tiles, 2, returned)
         with jax.named_scope("i_back"):
@@ -823,7 +824,8 @@
         for c in range(2):
             for y in range(2):
                 half = pl.ds(y * width, width)
-                out[0, c, :, half] += dot_lanes(same, flank_vel[c, y])
+                stay[c, :, half] += dot_lanes(same, flank_vel[c, y])
+        keep_here()
         wait_bytes(back.at[pl.ds(2, 1)], ret_ssem.at[0])
         wait_bytes(back.at[pl.ds(0, 2)], ret_ssem.at[1])
 
@@ -833,20 +835,18 @@
     peers = n_lat * n_lon
     f32 = jnp.float32
     anywhere = pl.BlockSpec(memory_space=pl.ANY)
-    in_vmem = pl.BlockSpec(memory_space=pltpu.VMEM)
     dma = pltpu.SemaphoreType.DMA
     halos = [pltpu.VMEM((2, num // 2, TILE, BX), f32) for _, num in ROUNDS] * 2
     sides = [pltpu.VMEM((2, TILE, BX), f32) for _ in ROUNDS]
     sides += [pltpu.VMEM((3, 2, TILE, BX), f32) for _ in ROUNDS]
-    return pl.pallas_call(
+    ret, here = pl.pallas_call(
         functools.partial(step_kernel, n_lat, n_lon),
-        out_shape=pltpu.VMEM((1, 2, count, cells), f32),
+        out_shape=(pltpu.VMEM((3, count, cells), f32), pltpu.VMEM((2, count, cells), f32)),
         in_specs=[anywhere, anywhere, anywhere, anywhere],
-        out_specs=in_vmem,
+        out_specs=(anywhere, anywhere),
         scratch_shapes=[
             pltpu.VMEM((7, count, cells), f32),
             pltpu.VMEM((2, count, cells), f32),
-            pltpu.VMEM((3, count, cells), f32),
             pltpu.VMEM((1, count), jnp.int32),
             pltpu.VMEM((1, count), jnp.int32),
             pltpu.VMEM((peers, 1, count), jnp.int32),
@@ -861,13 +861,15 @@
             pltpu.VMEM((2, 2, BX, count), f32),
             pltpu.VMEM((2, 2, BX, count), f32),
             *halos, *sides,
-            dma((4,)), dma, dma, dma((2,)), dma((2,)), dma((2,)), dma((2,)),
+            dma((5,)), dma, dma, dma((2,)), dma((2,)), dma((2,)), dma((2,)),
             dma((3, 10)), dma((3, 10)),
         ],
         compiler_params=pltpu.CompilerParams(
             collective_id=0, has_side_effects=True, vmem_limit_bytes=63 * 1024 * 1024
         ),
     )(fields, block_owner.reshape(1, count), ice_covered.reshape(1, count), land_mask)
+    is_ocean = lax.axis_index("comp") == 0
+    return jnp.where(is_ocean, ret[:2] + (1.0 - ret[2]) * here, here)[None]
 
 
 def solution(mesh):

time: 30.1 us -> 28.9 us (0.960)
  Pallas kernels: 29.2 us -> 28 us
  other arithmetic: 0 us -> 0.77 us
  local copies, waits for them, and re-layouts: 0.71 us -> 0 us
    pallas_call x1, Pallas kernels: 29.2 us -> 28 us  [per_device_kernel(): pl.pallas_call(functools.partial(step_kernel, n_lat, n_lon), out_shape=(p...]
    broadcast_in_dim x0 -> x1, other arithmetic: none -> 0.75 us  [per_device_kernel(): return jnp.where(is_ocean, ret[:2] + (1.0 - ret[2]) * here, here)[None]]
    unnamed x1 -> x0, local copies, waits for them, and re-layouts: 0.71 us -> none
where the time goes in v2:
time: 28.9 us; the launch traced here: 28.7 us
  Pallas kernels  28 us (97%)
  other arithmetic  0.77 us (3%)
    pallas_call x1, Pallas kernels, per_device_kernel(): pl.pallas_call(functools.partial(step_kernel, n_lat, n_lon), out_shape=(p...  28 us
    broadcast_in_dim x1, other arithmetic, per_device_kernel(): return jnp.where(is_ocean, ret[:2] + (1.0 - ret[2]) * here, here)[None]  0.75 us

profile of v2, /device:TPU:0, one launch (start us, length us, event | category | flops | bytes accessed | tf_op | source)
XLA Modules:
  0.0 28.7 jit_solution(9157109226477502899)
XLA Ops:
  0.0 28.0 %shard_map.46 = (f32[3,128,256]{2,1,0:T(8,128)S(1)}, f32[2,128,256]{2,1,0:T(8,128)S(1)}) custom-call(f32[1,7,128,256]{3,2,1,0:T(8,128)} %fields.1, s32[1,128]{1,0:T(1,128)} %bitcast.6, s32[1,128]{1,0:T(1,128)} %bitcast.7, s32[128,256]{1,0:T(8,128)} %land.1), custom_call_target="tpu_custom_call" | custom-call | tf_op jit(solution)/shard_map/pallas_call | solution.py:842
  28.0 0.8 %select_bitcast_fusion = f32[1,2,128,256]{3,2,1,0:T(8,128)} fusion(f32[2,128,256]{2,1,0:T(8,128)S(1)} %get-tuple-element.8, f32[3,128,256]{2,1,0:T(8,128)S(1)} %get-tuple-element.7, f32[128,256]{1,0:T(8,128)S(1)} %subtract_bitcast_fusion, pred[]{:T(512)S(6)} %eq.3), kind=kLoop, calls=%fused_computation | loop fusion | flops 196608 | bytes 917505 | tf_op jit(solution)/shard_map/broadcast_in_dim | solution.py:872
  (1 shorter events, 0.0 us)

commit v3 on v1

--- a/solution.py
+++ b/solution.py
@@ -198,7 +198,7 @@
 GROUP = 8
 MESH = pl.DeviceIdType.MESH
 U, V, MASS, CONC, S1, S2, S12, ACTIVE, PUSH_X, PUSH_Y, CUR_X, CUR_Y, STRENGTH, DRAG = range(14)
-SIDES = [(a, b) for b in (-1, 1) for a in (0, -1, 1)]
+SIDES = [(a, b) for b in (-1, 1) for a in (-1, 1, 0)]
 ALL_AROUND = [(-1, 0), (1, 0)] + SIDES
 ROUNDS = ((U, 8), (CUR_X, 2), (PUSH_X, 2))
 KEEP = 1.0 / (1.0 + RELAX)
@@ -213,25 +213,20 @@
 
 
 def pieces(values, axis):
-    parts = []
-    rest = values
-    for piece in range(3):
-        part = rest.astype(jnp.bfloat16)
-        if piece < 2:
-            rest = rest - part.astype(jnp.float32)
-        parts.append(part)
-    return jnp.concatenate(parts, axis=axis)
-
-
-def dot_rows(thrice, values):
+    high = values.astype(jnp.bfloat16)
+    low = (values - high.astype(jnp.float32)).astype(jnp.bfloat16)
+    return jnp.concatenate([high, low], axis=axis)
+
+
+def dot_rows(twice, values):
     return lax.dot_general(
-        thrice, pieces(values, 0), (((1,), (0,)), ((), ())), preferred_element_type=jnp.float32
-    )
-
-
-def dot_lanes(thrice, values):
+        twice, pieces(values, 0), (((1,), (0,)), ((), ())), preferred_element_type=jnp.float32
+    )
+
+
+def dot_lanes(twice, values):
     return lax.dot_general(
-        thrice, pieces(values, 1), (((1,), (1,)), ((), ())), preferred_element_type=jnp.float32
+        twice, pieces(values, 1), (((1,), (1,)), ((), ())), preferred_element_type=jnp.float32
     )
 
 
@@ -268,10 +263,11 @@
     n_lat, n_lon,
     fields, owner_hbm, covered_hbm, land, out,
     surf, open_st, ret, owner, covered, ids, recv, forc, one_hot, back, land_v,
-    main, edge, flank, flank_back, flank_vel,
+    main, edge, flank, flank_back, flank_vel, ends,
     rows_out0, rows_out1, rows_out2, rows_got0, rows_got1, rows_got2,
     side_out0, side_out1, side_out2, side_got0, side_got1, side_got2,
-    load_sem, ids_ssem, ids_rsem, fwd_ssem, fwd_rsem, ret_ssem, ret_rsem, halo_ssem, halo_rsem,
+    load_sem, ids_ssem, ids_rsem, fwd_ssem, fwd_rsem, ret_ssem, ret_rsem,
+    early_ssem, early_rsem, mid_rsem, late_rsem, later_ssem,
 ):
     comp = lax.axis_index("comp")
     lat = lax.axis_index("lat")
@@ -290,34 +286,37 @@
     def rows_of(peer):
         return pl.ds(pl.multiple_of(peer * per, per), per)
 
-    def device(kind, peer):
-        return (kind, peer // n_lon, peer % n_lon)
-
-    def each_peer(body):
-        def step(k, carry):
-            body((me + k) % peers)
-            return carry
-        lax.fori_loop(0, peers, step, 0)
+    planes = [(jnp.where(lat < n_lat // 2, n_lat // 2, 0) + j) % n_lat for j in range(n_lat)]
+    places = [(lon + i) % n_lon for i in range(n_lon)]
+
+    def each_peer(body, part=None):
+        chosen = {None: planes, 0: planes[:n_lat // 2], 1: planes[n_lat // 2:]}[part]
+        for plane in chosen:
+            for place in places:
+                body(plane * n_lon + place, plane, place)
 
     def signal_peers(kind):
         each_peer(
-            lambda p: pl.semaphore_signal(
-                barrier, inc=1, device_id=device(kind, p), device_id_type=MESH
+            lambda p, plane, place: pl.semaphore_signal(
+                barrier, inc=1, device_id=(kind, plane, place), device_id_type=MESH
             )
         )
 
-    def send_rows(kind, src, lo, num, dst, dlo, ssem, rsem):
-        def body(p):
+    def send_rows(kind, src, lo, num, dst, dlo, ssem, rsem, part=None):
+        def body(p, plane, place):
             pltpu.make_async_remote_copy(
                 src_ref=src.at[pl.ds(lo, num), rows_of(p), :],
                 dst_ref=dst.at[pl.ds(dlo, num), rows_of(me), :],
                 send_sem=ssem, recv_sem=rsem,
-                device_id=device(kind, p), device_id_type=MESH,
+                device_id=(kind, plane, place), device_id_type=MESH,
             ).start()
-        each_peer(body)
+        each_peer(body, part)
 
     def wait_bytes(ref, sem):
         pltpu.make_async_copy(ref, ref, sem).wait()
+
+    def wait_tiles(num, sem):
+        wait_bytes(main.at[0, 0, pl.ds(0, num * TILE), :], sem)
 
     @pl.when(comp == 0)
     def _ocean():
@@ -334,15 +333,15 @@
         with jax.named_scope("o_barrier"):
             pl.semaphore_wait(barrier, peers)
 
-        def ids_out(p):
+        def ids_out(p, plane, place):
             pltpu.make_async_remote_copy(
                 src_ref=owner, dst_ref=ids.at[me], send_sem=ids_ssem, recv_sem=ids_rsem,
-                device_id=device(1, p), device_id_type=MESH,
+                device_id=(1, plane, place), device_id_type=MESH,
             ).start()
         with jax.named_scope("o_send4"):
             each_peer(ids_out)
             raw.wait()
-            send_rows(1, surf, 2, 4, recv, 2, fwd_ssem.at[0], fwd_rsem.at[0])
+            send_rows(1, surf, 2, 4, recv, 2, fwd_ssem.at[0], fwd_rsem.at[0], 0)
             wind.wait()
             rho.wait()
 
@@ -354,8 +353,10 @@
             forc[1, r, :] = scale * wy
 
         with jax.named_scope("o_stress"):
-            tile_loop(count // TILE, 2, stress)
-            send_rows(1, forc, 0, 2, recv, 0, fwd_ssem.at[1], fwd_rsem.at[1])
+            tile_loop(count // TILE, 4, stress)
+            send_rows(1, forc, 0, 2, recv, 0, fwd_ssem.at[1], fwd_rsem.at[1], 0)
+            send_rows(1, surf, 2, 4, recv, 2, fwd_ssem.at[0], fwd_rsem.at[0], 1)
+            send_rows(1, forc, 0, 2, recv, 0, fwd_ssem.at[1], fwd_rsem.at[1], 1)
 
         def open_water(t):
             r = pl.ds(pl.multiple_of(t * TILE, TILE), TILE)
@@ -370,17 +371,23 @@
         tile_loop(count // TILE, 2, open_water)
         with jax.named_scope("o_waitret1"):
             wait_bytes(ret.at[pl.ds(2, 1)], ret_rsem.at[0])
+
+        def water(t):
+            r = pl.ds(pl.multiple_of(t * TILE, TILE), TILE)
+            share = 1.0 - ret[2, r, :]
+            for c in range(2):
+                open_st[c, r, :] = share * open_st[c, r, :]
+
+        tile_loop(count // TILE, 4, water)
         with jax.named_scope("o_waitret2"):
             wait_bytes(ret.at[pl.ds(0, 2)], ret_rsem.at[1])
 
         def finish(t):
             r = pl.ds(pl.multiple_of(t * TILE, TILE), TILE)
-            water = 1.0 - ret[2, r, :]
-            out[0, 0, r, :] = ret[0, r, :] + water * open_st[0, r, :]
-            out[0, 1, r, :] = ret[1, r, :] + water * open_st[1, r, :]
-
-        with jax.named_scope("o_finish"):
-            tile_loop(count // TILE, 2, finish)
+            for c in range(2):
+                out[0, c, r, :] = ret[c, r, :] + open_st[c, r, :]
+
+        tile_loop(count // TILE, 4, finish)
         wait_bytes(ids, ids_ssem)
         wait_bytes(surf.at[pl.ds(2, 4)], fwd_ssem.at[0])
         wait_bytes(forc.at[pl.ds(0, 2)], fwd_ssem.at[1])
@@ -427,8 +434,8 @@
             r = pl.ds(pl.multiple_of(t * TILE, TILE), TILE)
             for c in range(2):
                 for y in range(2):
-                    flank_back[c, y, r, :] = zero_tile
                     flank_vel[c, y, r, :] = zero_tile
+            flank_back[r, :] = zero_tile
 
         tile_loop(tiles, 2, clear)
         for load in loads:
@@ -449,11 +456,10 @@
         pick_col = lax.broadcasted_iota(jnp.int32, (2 * TILE, width), 1)
         picked = jnp.where(pick_row < TILE, pick_row, pick_row + (width - 2 * TILE)) == pick_col
         picker = jnp.where(picked, 1.0, 0.0).astype(jnp.bfloat16)
-        picker = jnp.concatenate([picker] * 3, axis=1)
-
-        def pack(e):
+        picker = jnp.concatenate([picker] * 2, axis=1)
+
+        def pack_rows(e):
             lo, num = ROUNDS[e]
-            west, east = zero_tile, zero_tile
             for k in range(num // 2):
                 ups, downs = zero_tile, zero_tile
                 for i in range(4):
@@ -462,59 +468,88 @@
                     here = (sub >= 2 * i) & (sub < 2 * i + 2)
                     ups = jnp.where(here, pltpu.roll(head, 2 * i, 0) if i else head, ups)
                     downs = jnp.where(here, pltpu.roll(foot, (2 * i + 2) % TILE, 0) if i < 3 else foot, downs)
-                    ends = jnp.where(sub < NSUB, head, foot)
-                    slot = (k * 4 + i) * NSUB
-                    mine = (lane >= slot) & (lane < slot + NSUB)
-                    west = jnp.where(mine, pltpu.roll(ends, slot, 1) if slot else ends, west)
-                    east = jnp.where(mine, pltpu.roll(ends, (slot + NSUB) % width, 1), east)
                 rows_out[e][0, k] = ups
                 rows_out[e][1, k] = downs
+
+        def pack_sides(e):
+            lo, num = ROUNDS[e]
+            west, east = zero_tile, zero_tile
+            for i in range(2 * num):
+                c, y = lo + i // 2, i % 2
+                ends = jnp.where(sub < NSUB, main[c, y, top, :], main[c, y, bottom, :])
+                slot = i * NSUB
+                mine = (lane >= slot) & (lane < slot + NSUB)
+                west = jnp.where(mine, pltpu.roll(ends, slot, 1) if slot else ends, west)
+                east = jnp.where(mine, pltpu.roll(ends, (slot + NSUB) % width, 1), east)
             side_out[e][0] = west
             side_out[e][1] = east
+
+        def pack_flank(e):
+            lo, num = ROUNDS[e]
             for c in range(lo, lo + num):
                 for y in range(2):
                     across = dot_lanes(picker, main[c, y])
                     flank[c, y, pl.ds(TILE, TILE), :] = across[:TILE]
                     flank[c, y, pl.ds(2 * TILE, TILE), :] = across[TILE:]
 
-        def halo(e, begin):
-            lo, num = ROUNDS[e]
-            moves = []
+        def push_on(e, a, b, src, dst, lane_of_sem, recv_lane):
+            sems = (early_rsem, mid_rsem, late_rsem)[e]
+            sent = early_ssem if e == 0 else later_ssem
+
+            @pl.when(inside(a))
+            def _():
+                pltpu.make_async_remote_copy(
+                    src_ref=src, dst_ref=dst,
+                    send_sem=sent.at[lane_of_sem], recv_sem=sems.at[recv_lane],
+                    device_id=around(a, b), device_id_type=MESH,
+                ).start()
+
+        def send_ends(e):
             for a in (-1, 1):
                 k = 1 if a > 0 else 0
-                moves.append((a, 0, rows_out[e].at[k], rows_got[e].at[1 - k]))
+                push_on(e, a, 0, rows_out[e].at[k], rows_got[e].at[1 - k], k, 1 - k)
+
+        def send_sides(e):
             for a, b in SIDES:
                 k = 1 if b > 0 else 0
-                moves.append((a, b, side_out[e].at[k], side_got[e].at[1 - a, 1 - k]))
+                group = {0: 2, -1: 0, 1: 1}[a]
+                land_in = {0: 2, -1: 1, 1: 0}[a] + (4 if e == 2 and a != 0 else 0)
+                push_on(e, a, b, side_out[e].at[k], side_got[e].at[1 - a, 1 - k], group, land_in)
+
+        def send_flank(e):
+            lo, num = ROUNDS[e]
             for b in (-1, 1):
                 src, dst = (2 * TILE, 0) if b > 0 else (TILE, 3 * TILE)
-                moves.append((
-                    0, b,
+                push_on(
+                    e, 0, b,
                     flank.at[pl.ds(lo, num), :, pl.ds(src, TILE), :],
-                    flank.at[pl.ds(lo, num), :, pl.ds(dst, TILE), :],
-                ))
-            for k, (a, b, src, dst) in enumerate(moves):
-                copy = pltpu.make_async_remote_copy(
-                    src_ref=src, dst_ref=dst,
-                    send_sem=halo_ssem.at[e, k], recv_sem=halo_rsem.at[e, k],
-                    device_id=around(a, b), device_id_type=MESH,
+                    flank.at[pl.ds(lo, num), :, pl.ds(dst, TILE), :], 3, 3,
                 )
-                if begin:
-                    @pl.when(inside(a))
-                    def _():
-                        copy.start()
-                else:
-                    @pl.when(inside(a))
-                    def _():
-                        copy.wait_send()
-
-                    @pl.when(inside(-a))
-                    def _():
-                        copy.wait_recv()
-
-        def unpack(e):
+
+        def when_inside(a, num, sem):
+            @pl.when(inside(a))
+            def _():
+                wait_tiles(num, sem)
+
+        def unpack_rows(e):
             lo, num = ROUNDS[e]
-            got, side = rows_got[e], side_got[e]
+            got = rows_got[e]
+            for k in range(num // 2):
+                for i in range(4):
+                    c, y = lo + 2 * k + i // 2, i % 2
+                    north = pltpu.roll(got[0, k], (TILE - 2 * i) % TILE, 0) if i else got[0, k]
+                    south = pltpu.roll(got[1, k], TILE - 2 - 2 * i, 0) if i < 3 else got[1, k]
+                    head, foot = main[c, y, top, :], main[c, y, bottom, :]
+                    edge[c, 0, y, :, pl.ds(0, width)] = jnp.where(
+                        sub < 2, north, pltpu.roll(head, 2, 0)
+                    )
+                    edge[c, 1, y, :, pl.ds(0, width)] = jnp.where(
+                        sub >= TILE - 2, south, pltpu.roll(foot, TILE - 2, 0)
+                    )
+
+        def unpack_sides(e):
+            lo, num = ROUNDS[e]
+            side = side_got[e]
             ends = []
             for k in range(2):
                 far, near = side[0, k], side[1, k]
@@ -522,26 +557,16 @@
             for k in range(2):
                 far, near = side[2, k], side[1, k]
                 ends.append(pltpu.roll(jnp.where(sub < 2, far, near), TILE - 2, 0))
-            for k in range(num // 2):
-                for i in range(4):
-                    c, y = lo + 2 * k + i // 2, i % 2
-                    slot = (k * 4 + i) * NSUB
-                    for strip in range(2):
-                        own = main[c, y, top if strip == 0 else bottom, :]
-                        beyond = got[strip, k]
-                        if strip == 0:
-                            beyond = pltpu.roll(beyond, (TILE - 2 * i) % TILE, 0) if i else beyond
-                            body = jnp.where(sub < 2, beyond, pltpu.roll(own, 2, 0))
-                        else:
-                            beyond = pltpu.roll(beyond, TILE - 2 - 2 * i, 0) if i < 3 else beyond
-                            body = jnp.where(sub >= TILE - 2, beyond, pltpu.roll(own, TILE - 2, 0))
-                        from_west, from_east = ends[2 * strip], ends[2 * strip + 1]
-                        from_east = pltpu.roll(from_east, width - slot, 1) if slot else from_east
-                        from_west = pltpu.roll(from_west, width - NSUB - slot, 1)
-                        edge[c, strip, y, :, pl.ds(0, width)] = body
-                        edge[c, strip, y, :, pl.ds(width, width)] = jnp.where(
-                            lane < NSUB, from_east, jnp.where(lane >= width - NSUB, from_west, 0.0)
-                        )
+            for i in range(2 * num):
+                c, y = lo + i // 2, i % 2
+                slot = i * NSUB
+                for strip in range(2):
+                    from_west, from_east = ends[2 * strip], ends[2 * strip + 1]
+                    from_east = pltpu.roll(from_east, width - slot, 1) if slot else from_east
+                    from_west = pltpu.roll(from_west, width - NSUB - slot, 1)
+                    edge[c, strip, y, :, pl.ds(width, width)] = jnp.where(
+                        lane < NSUB, from_east, jnp.where(lane >= width - NSUB, from_west, 0.0)
+                    )
 
         def derive(load, store):
             conc, act = load(CONC), load(ACTIVE)
@@ -623,13 +648,15 @@
                     main[V, y, r, :] = v
 
         def sweep_edge(stress, velocity):
+            lanes = 2 * width
+
             for strip in range(2):
                 vels = [(edge[U, strip, y], edge[V, strip, y]) for y in range(2)]
                 fresh = [tuple(edge[c, strip, y] for c in (S1, S2, S12)) for y in range(2)]
                 if stress:
                     ups = [vels[1], tuple(pltpu.roll(x, TILE - 1, 0) for x in vels[0])]
                     for y in range(2):
-                        east = [pltpu.roll(x, 2 * width - 1, 1) for x in vels[y]]
+                        east = [pltpu.roll(x, lanes - 1, 1) for x in vels[y]]
                         fresh[y] = new_stress(
                             edge[STRENGTH, strip, y], *fresh[y], *vels[y], *east, *ups[y]
                         )
@@ -695,8 +722,12 @@
         with jax.named_scope("i_barrier"):
             pl.semaphore_wait(barrier, peers + 8 - walls)
         with jax.named_scope("i_pack0"):
-            pack(0)
-            halo(0, True)
+            pack_rows(0)
+            pack_sides(0)
+            send_ends(0)
+            send_sides(0)
+            pack_flank(0)
+            send_flank(0)
         tile_loop(tiles, 2, derive_main)
 
         with jax.named_scope("i_waitids"):
@@ -713,9 +744,14 @@
             one_hot[pl.ds(p * per, per), :] = jnp.where(local == blocks, 1.0, 0.0)
 
         with jax.named_scope("i_waithalo0"):
-            halo(0, False)
+            for sems in (early_ssem, early_rsem):
+                when_inside(-1, 6, sems.at[0])
+                when_inside(1, 6, sems.at[1])
+                wait_tiles(2, sems.at[2])
+                wait_bytes(main.at[0], sems.at[3])
         with jax.named_scope("i_unpack0"):
-            unpack(0)
+            unpack_rows(0)
+            unpack_sides(0)
             derive_edges()
         groups = tiles // GROUP
         with jax.named_scope("i_stress"):
@@ -723,8 +759,12 @@
             sweep_edge(True, False)
             sweep_flank(True, False)
         by_slot = one_hot[...]
-        to_slots = jnp.concatenate([by_slot.astype(jnp.bfloat16)] * 3, axis=1)
-        to_blocks = jnp.concatenate([by_slot.T.astype(jnp.bfloat16)] * 3, axis=1)
+        to_slots = jnp.concatenate([by_slot.astype(jnp.bfloat16)] * 2, axis=1)
+        to_ends = jnp.concatenate([by_slot[:, :TILE], by_slot[:, count - TILE:]] * 2, axis=1)
+        to_ends = to_ends.astype(jnp.bfloat16)
+        by_block = by_slot.T.astype(jnp.bfloat16)
+        to_blocks = jnp.concatenate([by_block] * 2, axis=1)
+        columns = jnp.concatenate([by_block] * 2, axis=0)
 
         with jax.named_scope("i_waitf4"):
             wait_bytes(recv.at[pl.ds(2, 4)], fwd_rsem.at[0])
@@ -733,8 +773,12 @@
             for y in range(2):
                 main[CUR_X + c, y] = both[:, y * width:(y + 1) * width]
         with jax.named_scope("i_packmid"):
-            pack(1)
-            halo(1, True)
+            pack_rows(1)
+            pack_sides(1)
+            send_ends(1)
+            send_sides(1)
+            pack_flank(1)
+            send_flank(1)
         for c in range(2):
             both = dot_rows(to_blocks, recv[4 + c])
             for y in range(2):
@@ -742,7 +786,6 @@
         for y in range(2):
             share = main[CONC, y] * main[ACTIVE, y]
             back[2, :, pl.ds(y * width, width)] = dot_rows(to_slots, share)
-        send_rows(0, back, 2, 1, ret, 2, ret_ssem.at[0], ret_rsem.at[0])
 
         with jax.named_scope("i_waitf2"):
             wait_bytes(recv.at[pl.ds(0, 2)], fwd_rsem.at[1])
@@ -754,40 +797,69 @@
                         main[CONC, y] * both[:, y * width:(y + 1) * width] - main[PUSH_X + c, y]
                     )
         with jax.named_scope("i_packlate"):
-            pack(2)
-            halo(2, True)
+            pack_rows(2)
+            send_ends(2)
+            pack_sides(2)
+            send_sides(2)
+            pack_flank(2)
+            send_flank(2)
+
+        def leave(get, u, v):
+            dx, dy = u - get(CUR_X), v - get(CUR_Y)
+            drag = get(DRAG) * jnp.sqrt(dx * dx + dy * dy + DRAG_FLOOR)
+            return drag * dx, drag * dy
+
+        outer = (lane < NSUB) | (lane >= width - NSUB)
 
         with jax.named_scope("i_vel1"):
             tile_loop(groups, 1, lambda g: sweep_main(g, False, True))
         with jax.named_scope("i_sweeps"):
             tile_loop((NSUB - 1) * groups, 1, lambda k: sweep_main(k % groups, True, True))
+        send_rows(0, back, 2, 1, ret, 2, ret_ssem.at[0], ret_rsem.at[0])
+
+        def returned(t):
+            r = pl.ds(pl.multiple_of(t * TILE, TILE), TILE)
+            block = sub + t * TILE
+            theirs = outer | (block < 2) | (block >= count - 2)
+            for y in range(2):
+                half = pl.ds(y * width, width)
+                u, v = main[U, y, r, :], main[V, y, r, :]
+                gone = leave(lambda c: main[c, y, r, :], u, v)
+                for c in range(2):
+                    forc[c, r, half] = jnp.where(theirs, 0.0, gone[c])
+
+        with jax.named_scope("i_back"):
+            tile_loop(tiles, 4, returned)
+            for c in range(2):
+                back[c] = dot_rows(to_slots, forc[c])
         with jax.named_scope("i_waitmid"):
-            halo(1, False)
-        unpack(1)
+            when_inside(1, 3, mid_rsem.at[1])
+            when_inside(-1, 3, mid_rsem.at[0])
+            wait_tiles(2, mid_rsem.at[2])
+            wait_tiles(8, mid_rsem.at[3])
+        unpack_rows(1)
+        unpack_sides(1)
+        with jax.named_scope("i_waitrows"):
+            when_inside(-1, 1, late_rsem.at[0])
+            when_inside(1, 1, late_rsem.at[1])
+        unpack_rows(2)
         with jax.named_scope("i_waitlate"):
-            halo(2, False)
+            wait_tiles(2, late_rsem.at[2])
+            when_inside(-1, 2, late_rsem.at[4])
+            when_inside(1, 2, late_rsem.at[5])
+            wait_tiles(8, late_rsem.at[3])
+
+        def sweep_strips(stress, velocity):
+            sweep_flank(stress, velocity)
+            sweep_edge(stress, velocity)
+
         with jax.named_scope("i_edge"):
-            unpack(2)
-            sweep_edge(False, True)
-            tile_loop(NSUB - 1, 1, lambda k: sweep_edge(True, True))
-        with jax.named_scope("i_flank"):
-            sweep_flank(False, True)
-            tile_loop(NSUB - 1, 1, lambda k: sweep_flank(True, True))
-
-        def leave(get, u, v):
-            dx, dy = u - get(CUR_X), v - get(CUR_Y)
-            drag = get(DRAG) * jnp.sqrt(dx * dx + dy * dy + DRAG_FLOOR)
-            return drag * dx, drag * dy
-
-        outer = (lane < NSUB) | (lane >= width - NSUB)
-
-        with jax.named_scope("i_returned"):
+            unpack_sides(2)
+            sweep_strips(False, True)
+            tile_loop(NSUB - 1, 1, lambda k: sweep_strips(True, True))
+
+        with jax.named_scope("i_fix"):
             for y in range(2):
-                for c in (U, V):
-                    north = pltpu.roll(edge[c, 0, y, :, pl.ds(0, width)], TILE - 2, 0)
-                    south = pltpu.roll(edge[c, 1, y, :, pl.ds(0, width)], 2, 0)
-                    main[c, y, top, :] = jnp.where(sub < 2, north, main[c, y, top, :])
-                    main[c, y, bottom, :] = jnp.where(sub >= TILE - 2, south, main[c, y, bottom, :])
                 for j, far in ((1, 0), (2, count - TILE)):
                     r = pl.ds(j * TILE, TILE)
                     held = (lane >= 2) & (lane < count - 2)
@@ -795,37 +867,58 @@
                     u, v = flank[U, y, r, :], flank[V, y, r, :]
                     gone = leave(lambda c: flank[c, y, r, :], u, v)
                     for c in range(2):
-                        flank_back[c, y, pl.ds(far, TILE), :] = jnp.where(held, gone[c], 0.0)
+                        slot = (c * 2 + y) * 2 * TILE + (TILE if j == 1 else 0)
+                        flank_back[pl.ds(slot, TILE), :] = jnp.where(held, gone[c], 0.0)
                         flank_vel[c, y, pl.ds(far, TILE), :] = jnp.where(held, (u, v)[c], 0.0)
-
-            def returned(t):
-                r = pl.ds(pl.multiple_of(t * TILE, TILE), TILE)
-                block = sub + t * TILE
-                theirs = outer & (block >= 2) & (block < count - 2)
+                for strip in range(2):
+                    def get(c):
+                        return edge[c, strip, y, :, pl.ds(0, width)]
+                    gone = leave(get, get(U), get(V))
+                    held = (sub < 2) if strip == 0 else (sub >= TILE - 2)
+                    for c in range(2):
+                        moved = pltpu.roll(gone[c], TILE - 2 if strip == 0 else 2, 0)
+                        ends[c, pl.ds(strip * TILE, TILE), pl.ds(y * width, width)] = jnp.where(
+                            held, moved, 0.0
+                        )
+            across = lax.dot_general(
+                pieces(flank_back[...], 1), columns,
+                (((1,), (0,)), ((), ())), preferred_element_type=jnp.float32,
+            ).T
+            for c in range(2):
+                rest = dot_rows(to_ends, ends[c])
                 for y in range(2):
-                    half = pl.ds(y * width, width)
-                    u, v = main[U, y, r, :], main[V, y, r, :]
-                    gone = leave(lambda c: main[c, y, r, :], u, v)
-                    for c in range(2):
-                        forc[c, r, half] = jnp.where(theirs, 0.0, gone[c])
-                        out[0, c, r, half] = jnp.where(theirs, 0.0, (u, v)[c])
-
-            tile_loop(tiles, 2, returned)
-        with jax.named_scope("i_back"):
+                    slot = (c * 2 + y) * 2 * TILE
+                    for t in range(tiles):
+                        r, half = pl.ds(t * TILE, TILE), pl.ds(y * width, width)
+                        moved = pltpu.roll(across[t * TILE:(t + 1) * TILE], width - TILE - slot, 1)
+                        back[c, r, half] += jnp.where(outer, moved, 0.0) + (
+                            rest[t * TILE:(t + 1) * TILE, y * width:(y + 1) * width]
+                        )
+            send_rows(0, back, 0, 2, ret, 0, ret_ssem.at[1], ret_rsem.at[1])
+
+        same = jnp.where(diag, 1.0, 0.0).astype(jnp.bfloat16)
+        same = jnp.concatenate([same] * 2, axis=1)
+        for y in range(2):
             for c in range(2):
-                both = dot_rows(to_slots, forc[c])
-                for y in range(2):
-                    part = both[:, y * width:(y + 1) * width]
-                    back[c, :, pl.ds(y * width, width)] = part + dot_lanes(to_slots, flank_back[c, y])
-            send_rows(0, back, 0, 2, ret, 0, ret_ssem.at[1], ret_rsem.at[1])
-        same = jnp.where(diag, 1.0, 0.0).astype(jnp.bfloat16)
-        same = jnp.concatenate([same] * 3, axis=1)
-        for c in range(2):
-            for y in range(2):
                 half = pl.ds(y * width, width)
-                out[0, c, :, half] += dot_lanes(same, flank_vel[c, y])
+                for strip, r in ((0, top), (1, bottom)):
+                    end = pltpu.roll(
+                        edge[c, strip, y, :, pl.ds(0, width)], TILE - 2 if strip == 0 else 2, 0
+                    )
+                    held = (sub < 2) if strip == 0 else (sub >= TILE - 2)
+                    main[c, y, r, :] = jnp.where(held, end, main[c, y, r, :])
+                other = dot_lanes(same, flank_vel[c, y])
+                row = lax.broadcasted_iota(jnp.int32, (count, width), 0)
+                column = lax.broadcasted_iota(jnp.int32, (count, width), 1)
+                theirs = (row >= 2) & (row < count - 2)
+                theirs = theirs & ((column < NSUB) | (column >= width - NSUB))
+                out[0, c, :, half] = jnp.where(theirs, other, main[c, y])
         wait_bytes(back.at[pl.ds(2, 1)], ret_ssem.at[0])
         wait_bytes(back.at[pl.ds(0, 2)], ret_ssem.at[1])
+        when_inside(-1, 6, later_ssem.at[0])
+        when_inside(1, 6, later_ssem.at[1])
+        wait_tiles(4, later_ssem.at[2])
+        wait_tiles(16, later_ssem.at[3])
 
 
 def per_device_kernel(n_lat, n_lon, fields, block_owner, ice_covered, land_mask):
@@ -833,7 +926,6 @@
     peers = n_lat * n_lon
     f32 = jnp.float32
     anywhere = pl.BlockSpec(memory_space=pl.ANY)
-    in_vmem = pl.BlockSpec(memory_space=pltpu.VMEM)
     dma = pltpu.SemaphoreType.DMA
     halos = [pltpu.VMEM((2, num // 2, TILE, BX), f32) for _, num in ROUNDS] * 2
     sides = [pltpu.VMEM((2, TILE, BX), f32) for _ in ROUNDS]
@@ -842,7 +934,7 @@
         functools.partial(step_kernel, n_lat, n_lon),
         out_shape=pltpu.VMEM((1, 2, count, cells), f32),
         in_specs=[anywhere, anywhere, anywhere, anywhere],
-        out_specs=in_vmem,
+        out_specs=pl.BlockSpec(memory_space=pltpu.VMEM),
         scratch_shapes=[
             pltpu.VMEM((7, count, cells), f32),
             pltpu.VMEM((2, count, cells), f32),
@@ -858,11 +950,12 @@
             pltpu.VMEM((14, 2, count, BX), f32),
             pltpu.VMEM((14, 2, 2, TILE, 2 * BX), f32),
             pltpu.VMEM((14, 2, 4 * TILE, BX), f32),
+            pltpu.VMEM((BX, count), f32),
             pltpu.VMEM((2, 2, BX, count), f32),
-            pltpu.VMEM((2, 2, BX, count), f32),
+            pltpu.VMEM((2, 2 * TILE, cells), f32),
             *halos, *sides,
             dma((4,)), dma, dma, dma((2,)), dma((2,)), dma((2,)), dma((2,)),
-            dma((3, 10)), dma((3, 10)),
+            dma((4,)), dma((4,)), dma((4,)), dma((6,)), dma((4,)),
         ],
         compiler_params=pltpu.CompilerParams(
             collective_id=0, has_side_effects=True, vmem_limit_bytes=63 * 1024 * 1024

time: 30.1 us -> 28 us (0.930)
  Pallas kernels: 29.2 us -> 27.1 us
    pallas_call x1, Pallas kernels: 29.2 us -> 27.1 us  [per_device_kernel(): pl.pallas_call(functools.partial(step_kernel, n_lat, n_lon), out_shape=pl...]
where the time goes in v3:
time: 28 us; the launch traced here: 27.8 us
  Pallas kernels  27.1 us (97%)
  local copies, waits for them, and re-layouts  0.71 us (3%)
    pallas_call x1, Pallas kernels, per_device_kernel(): pl.pallas_call(functools.partial(step_kernel, n_lat, n_lon), out_shape=pl...  27.1 us
    unnamed x1, local copies, waits for them, and re-layouts  0.71 us

profile of v3, /device:TPU:0, one launch (start us, length us, event | category | flops | bytes accessed | tf_op | source)
XLA Modules:
  0.0 27.8 jit_solution(5141974552090681421)
XLA Ops:
  0.0 27.1 %shard_map.46 = f32[1,2,128,256]{3,2,1,0:T(8,128)S(1)} custom-call(f32[1,7,128,256]{3,2,1,0:T(8,128)} %fields.1, s32[1,128]{1,0:T(1,128)} %bitcast.2, s32[1,128]{1,0:T(1,128)} %bitcast.3, s32[128,256]{1,0:T(8,128)} %land.1), custom_call_target="tpu_custom_call" | custom-call | tf_op jit(solution)/shard_map/pallas_call | solution.py:933
  27.1 0.7 %copy.6 = f32[1,2,128,256]{3,2,1,0:T(8,128)} copy(f32[1,2,128,256]{3,2,1,0:T(8,128)S(1)} %shard_map.46) | data formatting | bytes 524288

commit v4 on v3

--- a/solution.py
+++ b/solution.py
@@ -199,7 +199,6 @@
 MESH = pl.DeviceIdType.MESH
 U, V, MASS, CONC, S1, S2, S12, ACTIVE, PUSH_X, PUSH_Y, CUR_X, CUR_Y, STRENGTH, DRAG = range(14)
 SIDES = [(a, b) for b in (-1, 1) for a in (-1, 1, 0)]
-ALL_AROUND = [(-1, 0), (1, 0)] + SIDES
 ROUNDS = ((U, 8), (CUR_X, 2), (PUSH_X, 2))
 KEEP = 1.0 / (1.0 + RELAX)
 
@@ -267,7 +266,7 @@
     rows_out0, rows_out1, rows_out2, rows_got0, rows_got1, rows_got2,
     side_out0, side_out1, side_out2, side_got0, side_got1, side_got2,
     load_sem, ids_ssem, ids_rsem, fwd_ssem, fwd_rsem, ret_ssem, ret_rsem,
-    early_ssem, early_rsem, mid_rsem, late_rsem, later_ssem,
+    early_ssem, early_rsem, mid_rsem, late_rsem, later_ssem, ready,
 ):
     comp = lax.axis_index("comp")
     lat = lax.axis_index("lat")
@@ -289,20 +288,29 @@
     planes = [(jnp.where(lat < n_lat // 2, n_lat // 2, 0) + j) % n_lat for j in range(n_lat)]
     places = [(lon + i) % n_lon for i in range(n_lon)]
 
-    def each_peer(body, part=None):
-        chosen = {None: planes, 0: planes[:n_lat // 2], 1: planes[n_lat // 2:]}[part]
-        for plane in chosen:
-            for place in places:
-                body(plane * n_lon + place, plane, place)
-
-    def signal_peers(kind):
+    half_lat = n_lat // 2
+    groups_of = {
+        "all": ((planes, places),),
+        "column": ((planes[:half_lat], places[:1]),),
+        "beyond": ((planes[:half_lat], places[1:]),),
+        "near": ((planes[half_lat:], places),),
+    }
+
+    def each_peer(body, part="all"):
+        for chosen, along in groups_of[part]:
+            for plane in chosen:
+                for place in along:
+                    body(plane * n_lon + place, plane, place)
+
+    def signal_peers(kind, part="all"):
         each_peer(
             lambda p, plane, place: pl.semaphore_signal(
                 barrier, inc=1, device_id=(kind, plane, place), device_id_type=MESH
-            )
+            ),
+            part,
         )
 
-    def send_rows(kind, src, lo, num, dst, dlo, ssem, rsem, part=None):
+    def send_rows(kind, src, lo, num, dst, dlo, ssem, rsem, part="all"):
         def body(p, plane, place):
             pltpu.make_async_remote_copy(
                 src_ref=src.at[pl.ds(lo, num), rows_of(p), :],
@@ -331,17 +339,23 @@
         rho.start()
         names.wait()
         with jax.named_scope("o_barrier"):
-            pl.semaphore_wait(barrier, peers)
+            pl.semaphore_wait(barrier, half_lat)
 
         def ids_out(p, plane, place):
             pltpu.make_async_remote_copy(
                 src_ref=owner, dst_ref=ids.at[me], send_sem=ids_ssem, recv_sem=ids_rsem,
                 device_id=(1, plane, place), device_id_type=MESH,
             ).start()
+
+        def send_four(part):
+            send_rows(1, surf, 2, 4, recv, 2, fwd_ssem.at[0], fwd_rsem.at[0], part)
+
+        def send_two(part):
+            send_rows(1, forc, 0, 2, recv, 0, fwd_ssem.at[1], fwd_rsem.at[1], part)
+
         with jax.named_scope("o_send4"):
-            each_peer(ids_out)
             raw.wait()
-            send_rows(1, surf, 2, 4, recv, 2, fwd_ssem.at[0], fwd_rsem.at[0], 0)
+            send_four("column")
             wind.wait()
             rho.wait()
 
@@ -354,9 +368,15 @@
 
         with jax.named_scope("o_stress"):
             tile_loop(count // TILE, 4, stress)
-            send_rows(1, forc, 0, 2, recv, 0, fwd_ssem.at[1], fwd_rsem.at[1], 0)
-            send_rows(1, surf, 2, 4, recv, 2, fwd_ssem.at[0], fwd_rsem.at[0], 1)
-            send_rows(1, forc, 0, 2, recv, 0, fwd_ssem.at[1], fwd_rsem.at[1], 1)
+            send_two("column")
+        with jax.named_scope("o_ready"):
+            pl.semaphore_wait(ready, 1)
+        with jax.named_scope("o_rest"):
+            each_peer(ids_out)
+            send_four("beyond")
+            send_two("beyond")
+            send_four("near")
+            send_two("near")
 
         def open_water(t):
             r = pl.ds(pl.multiple_of(t * TILE, TILE), TILE)
@@ -402,11 +422,14 @@
         def around(a, b):
             return (1, lat + a, (lon + b + n_lon) % n_lon)
 
-        signal_peers(0)
-        for a, b in ALL_AROUND:
-            @pl.when(inside(a))
-            def _():
-                pl.semaphore_signal(barrier, inc=1, device_id=around(a, b), device_id_type=MESH)
+        signal_peers(0, "column")
+        for a in range(n_lat):
+            for b in range(n_lon):
+                if a or b:
+                    pl.semaphore_signal(
+                        barrier, inc=1, device_id=(1, (lat + a) % n_lat, (lon + b) % n_lon),
+                        device_id_type=MESH,
+                    )
         loads = [
             pltpu.make_async_copy(
                 fields.at[0, :, :, pl.ds(y * width, width)], main.at[pl.ds(0, 7), y], load_sem.at[y]
@@ -417,6 +440,9 @@
         loads.append(pltpu.make_async_copy(covered_hbm, covered, load_sem.at[3]))
         for load in loads:
             load.start()
+        with jax.named_scope("i_barrier"):
+            pl.semaphore_wait(barrier, 2 * peers - 1)
+            pl.semaphore_signal(ready, inc=1, device_id=(0, lat, lon), device_id_type=MESH)
 
         tiles = count // TILE
         top, bottom = pl.ds(0, TILE), pl.ds(count - TILE, TILE)
@@ -718,9 +744,6 @@
                     flank[U, y, r, :] = u
                     flank[V, y, r, :] = v
 
-        walls = jnp.where(lat == 0, 3, 0) + jnp.where(lat == n_lat - 1, 3, 0)
-        with jax.named_scope("i_barrier"):
-            pl.semaphore_wait(barrier, peers + 8 - walls)
         with jax.named_scope("i_pack0"):
             pack_rows(0)
             pack_sides(0)
@@ -956,6 +979,7 @@
             *halos, *sides,
             dma((4,)), dma, dma, dma((2,)), dma((2,)), dma((2,)), dma((2,)),
             dma((4,)), dma((4,)), dma((4,)), dma((6,)), dma((4,)),
+            pltpu.SemaphoreType.REGULAR,
         ],
         compiler_params=pltpu.CompilerParams(
             collective_id=0, has_side_effects=True, vmem_limit_bytes=63 * 1024 * 1024

time: 28 us -> 27.3 us (0.975)
  Pallas kernels: 27.1 us -> 26.4 us
    pallas_call x1, Pallas kernels: 27.1 us -> 26.4 us  [per_device_kernel(): pl.pallas_call(functools.partial(step_kernel, n_lat, n_lon), out_shape=pl...]
where the time goes in v4:
time: 27.3 us; the launch traced here: 27.2 us
  Pallas kernels  26.4 us (97%)
  local copies, waits for them, and re-layouts  0.71 us (3%)
    pallas_call x1, Pallas kernels, per_device_kernel(): pl.pallas_call(functools.partial(step_kernel, n_lat, n_lon), out_shape=pl...  26.4 us
    unnamed x1, local copies, waits for them, and re-layouts  0.71 us

profile of v4, /device:TPU:0, one launch (start us, length us, event | category | flops | bytes accessed | tf_op | source)
XLA Modules:
  0.0 27.2 jit_solution(10885919546994471635)
XLA Ops:
  0.0 26.4 %shard_map.46 = f32[1,2,128,256]{3,2,1,0:T(8,128)S(1)} custom-call(f32[1,7,128,256]{3,2,1,0:T(8,128)} %fields.1, s32[1,128]{1,0:T(1,128)} %bitcast.2, s32[1,128]{1,0:T(1,128)} %bitcast.3, s32[128,256]{1,0:T(8,128)} %land.1), custom_call_target="tpu_custom_call" | custom-call | tf_op jit(solution)/shard_map/pallas_call | solution.py:956
  26.4 0.7 %copy.6 = f32[1,2,128,256]{3,2,1,0:T(8,128)} copy(f32[1,2,128,256]{3,2,1,0:T(8,128)S(1)} %shard_map.46) | data formatting | bytes 524288

commit v5 on v4

--- a/solution.py
+++ b/solution.py
@@ -266,7 +266,7 @@
     rows_out0, rows_out1, rows_out2, rows_got0, rows_got1, rows_got2,
     side_out0, side_out1, side_out2, side_got0, side_got1, side_got2,
     load_sem, ids_ssem, ids_rsem, fwd_ssem, fwd_rsem, ret_ssem, ret_rsem,
-    early_ssem, early_rsem, mid_rsem, late_rsem, later_ssem, ready,
+    halo_ssem, early_rsem, later_rsem, ready,
 ):
     comp = lax.axis_index("comp")
     lat = lax.axis_index("lat")
@@ -285,7 +285,7 @@
     def rows_of(peer):
         return pl.ds(pl.multiple_of(peer * per, per), per)
 
-    planes = [(jnp.where(lat < n_lat // 2, n_lat // 2, 0) + j) % n_lat for j in range(n_lat)]
+    planes = [jnp.where(lat < n_lat // 2, n_lat - 1 - j, j) for j in range(n_lat)]
     places = [(lon + i) % n_lon for i in range(n_lon)]
 
     half_lat = n_lat // 2
@@ -329,29 +329,20 @@
     @pl.when(comp == 0)
     def _ocean():
         signal_peers(1)
-        names = pltpu.make_async_copy(owner_hbm, owner, load_sem.at[3])
         raw = pltpu.make_async_copy(fields.at[0, pl.ds(2, 4)], surf.at[pl.ds(2, 4)], load_sem.at[0])
         wind = pltpu.make_async_copy(fields.at[0, pl.ds(0, 2)], surf.at[pl.ds(0, 2)], load_sem.at[1])
         rho = pltpu.make_async_copy(fields.at[0, pl.ds(6, 1)], surf.at[pl.ds(6, 1)], load_sem.at[2])
-        names.start()
         raw.start()
         wind.start()
         rho.start()
-        names.wait()
         with jax.named_scope("o_barrier"):
             pl.semaphore_wait(barrier, half_lat)
 
-        def ids_out(p, plane, place):
-            pltpu.make_async_remote_copy(
-                src_ref=owner, dst_ref=ids.at[me], send_sem=ids_ssem, recv_sem=ids_rsem,
-                device_id=(1, plane, place), device_id_type=MESH,
-            ).start()
-
         def send_four(part):
-            send_rows(1, surf, 2, 4, recv, 2, fwd_ssem.at[0], fwd_rsem.at[0], part)
+            send_rows(1, surf, 2, 4, recv, 2, fwd_ssem, fwd_rsem.at[0], part)
 
         def send_two(part):
-            send_rows(1, forc, 0, 2, recv, 0, fwd_ssem.at[1], fwd_rsem.at[1], part)
+            send_rows(1, forc, 0, 2, recv, 0, fwd_ssem, fwd_rsem.at[1], part)
 
         with jax.named_scope("o_send4"):
             raw.wait()
@@ -372,7 +363,6 @@
         with jax.named_scope("o_ready"):
             pl.semaphore_wait(ready, 1)
         with jax.named_scope("o_rest"):
-            each_peer(ids_out)
             send_four("beyond")
             send_two("beyond")
             send_four("near")
@@ -408,9 +398,7 @@
                 out[0, c, r, :] = ret[c, r, :] + open_st[c, r, :]
 
         tile_loop(count // TILE, 4, finish)
-        wait_bytes(ids, ids_ssem)
-        wait_bytes(surf.at[pl.ds(2, 4)], fwd_ssem.at[0])
-        wait_bytes(forc.at[pl.ds(0, 2)], fwd_ssem.at[1])
+        wait_bytes(surf.at[pl.ds(0, 6)], fwd_ssem)
 
     @pl.when(comp == 1)
     def _ice():
@@ -438,11 +426,23 @@
         ]
         loads.append(pltpu.make_async_copy(land, land_v, load_sem.at[2]))
         loads.append(pltpu.make_async_copy(covered_hbm, covered, load_sem.at[3]))
+        names = pltpu.make_async_copy(owner_hbm, owner, load_sem.at[4])
+        names.start()
         for load in loads:
             load.start()
         with jax.named_scope("i_barrier"):
             pl.semaphore_wait(barrier, 2 * peers - 1)
             pl.semaphore_signal(ready, inc=1, device_id=(0, lat, lon), device_id_type=MESH)
+            names.wait()
+            for a in range(n_lat):
+                for b in range(n_lon):
+                    if a or b:
+                        pltpu.make_async_remote_copy(
+                            src_ref=owner, dst_ref=ids.at[me], send_sem=ids_ssem, recv_sem=ids_rsem,
+                            device_id=(1, (lat + a) % n_lat, (lon + b) % n_lon),
+                            device_id_type=MESH,
+                        ).start()
+        ids[me] = owner[...]
 
         tiles = count // TILE
         top, bottom = pl.ds(0, TILE), pl.ds(count - TILE, TILE)
@@ -519,14 +519,13 @@
                     flank[c, y, pl.ds(2 * TILE, TILE), :] = across[TILE:]
 
         def push_on(e, a, b, src, dst, lane_of_sem, recv_lane):
-            sems = (early_rsem, mid_rsem, late_rsem)[e]
-            sent = early_ssem if e == 0 else later_ssem
+            sems = early_rsem if e == 0 else later_rsem
 
             @pl.when(inside(a))
             def _():
                 pltpu.make_async_remote_copy(
                     src_ref=src, dst_ref=dst,
-                    send_sem=sent.at[lane_of_sem], recv_sem=sems.at[recv_lane],
+                    send_sem=halo_ssem.at[lane_of_sem], recv_sem=sems.at[recv_lane],
                     device_id=around(a, b), device_id_type=MESH,
                 ).start()
 
@@ -539,7 +538,7 @@
             for a, b in SIDES:
                 k = 1 if b > 0 else 0
                 group = {0: 2, -1: 0, 1: 1}[a]
-                land_in = {0: 2, -1: 1, 1: 0}[a] + (4 if e == 2 and a != 0 else 0)
+                land_in = {0: 2, -1: 1, 1: 0}[a]
                 push_on(e, a, b, side_out[e].at[k], side_got[e].at[1 - a, 1 - k], group, land_in)
 
         def send_flank(e):
@@ -754,7 +753,7 @@
         tile_loop(tiles, 2, derive_main)
 
         with jax.named_scope("i_waitids"):
-            wait_bytes(ids, ids_rsem)
+            wait_bytes(ids.at[pl.ds(0, peers - 1)], ids_rsem)
         wanted = me * per
         row_lane = lax.broadcasted_iota(jnp.int32, (per, count), 1)
         row_sub = lax.broadcasted_iota(jnp.int32, (per, count), 0)
@@ -767,7 +766,7 @@
             one_hot[pl.ds(p * per, per), :] = jnp.where(local == blocks, 1.0, 0.0)
 
         with jax.named_scope("i_waithalo0"):
-            for sems in (early_ssem, early_rsem):
+            for sems in (halo_ssem, early_rsem):
                 when_inside(-1, 6, sems.at[0])
                 when_inside(1, 6, sems.at[1])
                 wait_tiles(2, sems.at[2])
@@ -820,12 +819,12 @@
                         main[CONC, y] * both[:, y * width:(y + 1) * width] - main[PUSH_X + c, y]
                     )
         with jax.named_scope("i_packlate"):
-            pack_rows(2)
-            send_ends(2)
             pack_sides(2)
             send_sides(2)
             pack_flank(2)
             send_flank(2)
+            pack_rows(2)
+            send_ends(2)
 
         def leave(get, u, v):
             dx, dy = u - get(CUR_X), v - get(CUR_Y)
@@ -838,7 +837,7 @@
             tile_loop(groups, 1, lambda g: sweep_main(g, False, True))
         with jax.named_scope("i_sweeps"):
             tile_loop((NSUB - 1) * groups, 1, lambda k: sweep_main(k % groups, True, True))
-        send_rows(0, back, 2, 1, ret, 2, ret_ssem.at[0], ret_rsem.at[0])
+        send_rows(0, back, 2, 1, ret, 2, ret_ssem, ret_rsem.at[0])
 
         def returned(t):
             r = pl.ds(pl.multiple_of(t * TILE, TILE), TILE)
@@ -855,31 +854,23 @@
             tile_loop(tiles, 4, returned)
             for c in range(2):
                 back[c] = dot_rows(to_slots, forc[c])
-        with jax.named_scope("i_waitmid"):
-            when_inside(1, 3, mid_rsem.at[1])
-            when_inside(-1, 3, mid_rsem.at[0])
-            wait_tiles(2, mid_rsem.at[2])
-            wait_tiles(8, mid_rsem.at[3])
-        unpack_rows(1)
-        unpack_sides(1)
-        with jax.named_scope("i_waitrows"):
-            when_inside(-1, 1, late_rsem.at[0])
-            when_inside(1, 1, late_rsem.at[1])
-        unpack_rows(2)
         with jax.named_scope("i_waitlate"):
-            wait_tiles(2, late_rsem.at[2])
-            when_inside(-1, 2, late_rsem.at[4])
-            when_inside(1, 2, late_rsem.at[5])
-            wait_tiles(8, late_rsem.at[3])
+            when_inside(-1, 6, later_rsem.at[0])
+            when_inside(1, 6, later_rsem.at[1])
+            wait_tiles(4, later_rsem.at[2])
+            wait_tiles(16, later_rsem.at[3])
 
         def sweep_strips(stress, velocity):
             sweep_flank(stress, velocity)
             sweep_edge(stress, velocity)
 
         with jax.named_scope("i_edge"):
-            unpack_sides(2)
+            for e in (1, 2):
+                unpack_rows(e)
+                unpack_sides(e)
             sweep_strips(False, True)
-            tile_loop(NSUB - 1, 1, lambda k: sweep_strips(True, True))
+            for _ in range(NSUB - 1):
+                sweep_strips(True, True)
 
         with jax.named_scope("i_fix"):
             for y in range(2):
@@ -917,7 +908,7 @@
                         back[c, r, half] += jnp.where(outer, moved, 0.0) + (
                             rest[t * TILE:(t + 1) * TILE, y * width:(y + 1) * width]
                         )
-            send_rows(0, back, 0, 2, ret, 0, ret_ssem.at[1], ret_rsem.at[1])
+            send_rows(0, back, 0, 2, ret, 0, ret_ssem, ret_rsem.at[1])
 
         same = jnp.where(diag, 1.0, 0.0).astype(jnp.bfloat16)
         same = jnp.concatenate([same] * 2, axis=1)
@@ -936,12 +927,12 @@
                 theirs = (row >= 2) & (row < count - 2)
                 theirs = theirs & ((column < NSUB) | (column >= width - NSUB))
                 out[0, c, :, half] = jnp.where(theirs, other, main[c, y])
-        wait_bytes(back.at[pl.ds(2, 1)], ret_ssem.at[0])
-        wait_bytes(back.at[pl.ds(0, 2)], ret_ssem.at[1])
-        when_inside(-1, 6, later_ssem.at[0])
-        when_inside(1, 6, later_ssem.at[1])
-        wait_tiles(4, later_ssem.at[2])
-        wait_tiles(16, later_ssem.at[3])
+        wait_bytes(ids.at[pl.ds(0, peers - 1)], ids_ssem)
+        wait_bytes(back, ret_ssem)
+        when_inside(-1, 6, halo_ssem.at[0])
+        when_inside(1, 6, halo_ssem.at[1])
+        wait_tiles(4, halo_ssem.at[2])
+        wait_tiles(16, halo_ssem.at[3])
 
 
 def per_device_kernel(n_lat, n_lon, fields, block_owner, ice_covered, land_mask):
@@ -977,8 +968,8 @@
             pltpu.VMEM((2, 2, BX, count), f32),
             pltpu.VMEM((2, 2 * TILE, cells), f32),
             *halos, *sides,
-            dma((4,)), dma, dma, dma((2,)), dma((2,)), dma((2,)), dma((2,)),
-            dma((4,)), dma((4,)), dma((4,)), dma((6,)), dma((4,)),
+            dma((5,)), dma, dma, dma, dma((2,)), dma, dma((2,)),
+            dma((4,)), dma((4,)), dma((4,)),
             pltpu.SemaphoreType.REGULAR,
         ],
         compiler_params=pltpu.CompilerParams(

time: 27.3 us -> 26.7 us (0.978)
  Pallas kernels: 26.4 us -> 25.8 us
    pallas_call x1, Pallas kernels: 26.4 us -> 25.8 us  [per_device_kernel(): pl.pallas_call(functools.partial(step_kernel, n_lat, n_lon), out_shape=pl...]
where the time goes in v5:
time: 26.7 us; the launch traced here: 26.5 us
  Pallas kernels  25.8 us (97%)
  local copies, waits for them, and re-layouts  0.71 us (3%)
    pallas_call x1, Pallas kernels, per_device_kernel(): pl.pallas_call(functools.partial(step_kernel, n_lat, n_lon), out_shape=pl...  25.8 us
    unnamed x1, local copies, waits for them, and re-layouts  0.71 us

profile of v5, /device:TPU:0, one launch (start us, length us, event | category | flops | bytes accessed | tf_op | source)
XLA Modules:
  0.0 26.5 jit_solution(6066729774717518079)
XLA Ops:
  0.0 25.8 %shard_map.46 = f32[1,2,128,256]{3,2,1,0:T(8,128)S(1)} custom-call(f32[1,7,128,256]{3,2,1,0:T(8,128)} %fields.1, s32[1,128]{1,0:T(1,128)} %bitcast.2, s32[1,128]{1,0:T(1,128)} %bitcast.3, s32[128,256]{1,0:T(8,128)} %land.1), custom_call_target="tpu_custom_call" | custom-call | tf_op jit(solution)/shard_map/pallas_call | solution.py:947
  25.8 0.7 %copy.6 = f32[1,2,128,256]{3,2,1,0:T(8,128)} copy(f32[1,2,128,256]{3,2,1,0:T(8,128)S(1)} %shard_map.46) | data formatting | bytes 524288

commit v6 on v5

--- a/solution.py
+++ b/solution.py
@@ -262,11 +262,10 @@
     n_lat, n_lon,
     fields, owner_hbm, covered_hbm, land, out,
     surf, open_st, ret, owner, covered, ids, recv, forc, one_hot, back, land_v,
-    main, edge, flank, flank_back, flank_vel, ends,
+    main, edge, flank, flank_back, flank_vel, ends, near_push,
     rows_out0, rows_out1, rows_out2, rows_got0, rows_got1, rows_got2,
     side_out0, side_out1, side_out2, side_got0, side_got1, side_got2,
-    load_sem, ids_ssem, ids_rsem, fwd_ssem, fwd_rsem, ret_ssem, ret_rsem,
-    halo_ssem, early_rsem, later_rsem, ready,
+    bulk_ssem, bulk_rsem, ids_ssem, ids_rsem, halo_ssem, early_rsem, mid_rsem, late_rsem, ready,
 ):
     comp = lax.axis_index("comp")
     lat = lax.axis_index("lat")
@@ -302,6 +301,17 @@
                 for place in along:
                     body(plane * n_lon + place, plane, place)
 
+    def home_first(body):
+        body(0, 0, 0)
+        for plane in range(n_lat):
+            for place in places:
+                if plane:
+                    body(plane * n_lon + place, plane, place)
+                else:
+                    @pl.when(place > 0)
+                    def _():
+                        body(place, 0, place)
+
     def signal_peers(kind, part="all"):
         each_peer(
             lambda p, plane, place: pl.semaphore_signal(
@@ -318,7 +328,7 @@
                 send_sem=ssem, recv_sem=rsem,
                 device_id=(kind, plane, place), device_id_type=MESH,
             ).start()
-        each_peer(body, part)
+        home_first(body) if part == "home" else each_peer(body, part)
 
     def wait_bytes(ref, sem):
         pltpu.make_async_copy(ref, ref, sem).wait()
@@ -329,9 +339,9 @@
     @pl.when(comp == 0)
     def _ocean():
         signal_peers(1)
-        raw = pltpu.make_async_copy(fields.at[0, pl.ds(2, 4)], surf.at[pl.ds(2, 4)], load_sem.at[0])
-        wind = pltpu.make_async_copy(fields.at[0, pl.ds(0, 2)], surf.at[pl.ds(0, 2)], load_sem.at[1])
-        rho = pltpu.make_async_copy(fields.at[0, pl.ds(6, 1)], surf.at[pl.ds(6, 1)], load_sem.at[2])
+        raw = pltpu.make_async_copy(fields.at[0, pl.ds(2, 4)], surf.at[pl.ds(2, 4)], halo_ssem.at[0])
+        wind = pltpu.make_async_copy(fields.at[0, pl.ds(0, 2)], surf.at[pl.ds(0, 2)], halo_ssem.at[1])
+        rho = pltpu.make_async_copy(fields.at[0, pl.ds(6, 1)], surf.at[pl.ds(6, 1)], halo_ssem.at[2])
         raw.start()
         wind.start()
         rho.start()
@@ -339,10 +349,10 @@
             pl.semaphore_wait(barrier, half_lat)
 
         def send_four(part):
-            send_rows(1, surf, 2, 4, recv, 2, fwd_ssem, fwd_rsem.at[0], part)
+            send_rows(1, surf, 2, 4, recv, 2, bulk_ssem, bulk_rsem.at[0], part)
 
         def send_two(part):
-            send_rows(1, forc, 0, 2, recv, 0, fwd_ssem, fwd_rsem.at[1], part)
+            send_rows(1, forc, 0, 2, recv, 0, bulk_ssem, bulk_rsem.at[1], part)
 
         with jax.named_scope("o_send4"):
             raw.wait()
@@ -380,7 +390,7 @@
 
         tile_loop(count // TILE, 2, open_water)
         with jax.named_scope("o_waitret1"):
-            wait_bytes(ret.at[pl.ds(2, 1)], ret_rsem.at[0])
+            wait_bytes(ret.at[pl.ds(2, 1)], bulk_rsem.at[0])
 
         def water(t):
             r = pl.ds(pl.multiple_of(t * TILE, TILE), TILE)
@@ -390,7 +400,7 @@
 
         tile_loop(count // TILE, 4, water)
         with jax.named_scope("o_waitret2"):
-            wait_bytes(ret.at[pl.ds(0, 2)], ret_rsem.at[1])
+            wait_bytes(ret.at[pl.ds(0, 2)], bulk_rsem.at[1])
 
         def finish(t):
             r = pl.ds(pl.multiple_of(t * TILE, TILE), TILE)
@@ -398,7 +408,7 @@
                 out[0, c, r, :] = ret[c, r, :] + open_st[c, r, :]
 
         tile_loop(count // TILE, 4, finish)
-        wait_bytes(surf.at[pl.ds(0, 6)], fwd_ssem)
+        wait_bytes(surf.at[pl.ds(0, 6)], bulk_ssem)
 
     @pl.when(comp == 1)
     def _ice():
@@ -418,15 +428,15 @@
                         barrier, inc=1, device_id=(1, (lat + a) % n_lat, (lon + b) % n_lon),
                         device_id_type=MESH,
                     )
+        for y in range(2):
+            pltpu.make_async_copy(
+                fields.at[0, :, :, pl.ds(y * width, width)], main.at[pl.ds(0, 7), y], halo_ssem.at[0]
+            ).start()
         loads = [
-            pltpu.make_async_copy(
-                fields.at[0, :, :, pl.ds(y * width, width)], main.at[pl.ds(0, 7), y], load_sem.at[y]
-            )
-            for y in range(2)
+            pltpu.make_async_copy(land, land_v, halo_ssem.at[1]),
+            pltpu.make_async_copy(covered_hbm, covered, halo_ssem.at[2]),
         ]
-        loads.append(pltpu.make_async_copy(land, land_v, load_sem.at[2]))
-        loads.append(pltpu.make_async_copy(covered_hbm, covered, load_sem.at[3]))
-        names = pltpu.make_async_copy(owner_hbm, owner, load_sem.at[4])
+        names = pltpu.make_async_copy(owner_hbm, owner, halo_ssem.at[3])
         names.start()
         for load in loads:
             load.start()
@@ -464,6 +474,7 @@
             flank_back[r, :] = zero_tile
 
         tile_loop(tiles, 2, clear)
+        wait_bytes(main.at[pl.ds(0, 7)], halo_ssem.at[0])
         for load in loads:
             load.wait()
         diag = lax.broadcasted_iota(jnp.int32, (count, count), 0) == lax.broadcasted_iota(
@@ -484,13 +495,18 @@
         picker = jnp.where(picked, 1.0, 0.0).astype(jnp.bfloat16)
         picker = jnp.concatenate([picker] * 2, axis=1)
 
+        def end_of(e, c, y, k):
+            if e == 2:
+                return near_push[c - PUSH_X, y, k]
+            return main[c, y, (top, bottom)[k], :]
+
         def pack_rows(e):
             lo, num = ROUNDS[e]
             for k in range(num // 2):
                 ups, downs = zero_tile, zero_tile
                 for i in range(4):
                     c, y = lo + 2 * k + i // 2, i % 2
-                    head, foot = main[c, y, top, :], main[c, y, bottom, :]
+                    head, foot = end_of(e, c, y, 0), end_of(e, c, y, 1)
                     here = (sub >= 2 * i) & (sub < 2 * i + 2)
                     ups = jnp.where(here, pltpu.roll(head, 2 * i, 0) if i else head, ups)
                     downs = jnp.where(here, pltpu.roll(foot, (2 * i + 2) % TILE, 0) if i < 3 else foot, downs)
@@ -502,7 +518,7 @@
             west, east = zero_tile, zero_tile
             for i in range(2 * num):
                 c, y = lo + i // 2, i % 2
-                ends = jnp.where(sub < NSUB, main[c, y, top, :], main[c, y, bottom, :])
+                ends = jnp.where(sub < NSUB, end_of(e, c, y, 0), end_of(e, c, y, 1))
                 slot = i * NSUB
                 mine = (lane >= slot) & (lane < slot + NSUB)
                 west = jnp.where(mine, pltpu.roll(ends, slot, 1) if slot else ends, west)
@@ -519,7 +535,7 @@
                     flank[c, y, pl.ds(2 * TILE, TILE), :] = across[TILE:]
 
         def push_on(e, a, b, src, dst, lane_of_sem, recv_lane):
-            sems = early_rsem if e == 0 else later_rsem
+            sems = (early_rsem, mid_rsem, late_rsem)[e]
 
             @pl.when(inside(a))
             def _():
@@ -786,10 +802,11 @@
         to_ends = to_ends.astype(jnp.bfloat16)
         by_block = by_slot.T.astype(jnp.bfloat16)
         to_blocks = jnp.concatenate([by_block] * 2, axis=1)
+        end_blocks = jnp.concatenate([to_blocks[:TILE], to_blocks[count - TILE:]], axis=0)
         columns = jnp.concatenate([by_block] * 2, axis=0)
 
         with jax.named_scope("i_waitf4"):
-            wait_bytes(recv.at[pl.ds(2, 4)], fwd_rsem.at[0])
+            wait_bytes(recv.at[pl.ds(2, 4)], bulk_rsem.at[0])
         for c in range(2):
             both = dot_rows(to_blocks, recv[2 + c])
             for y in range(2):
@@ -810,21 +827,33 @@
             back[2, :, pl.ds(y * width, width)] = dot_rows(to_slots, share)
 
         with jax.named_scope("i_waitf2"):
-            wait_bytes(recv.at[pl.ds(0, 2)], fwd_rsem.at[1])
+            wait_bytes(recv.at[pl.ds(0, 2)], bulk_rsem.at[1])
         with jax.named_scope("i_push"):
+            for c in range(2):
+                both = lax.dot_general(
+                    end_blocks, pieces(recv[c], 0), (((1,), (0,)), ((), ())),
+                    preferred_element_type=jnp.float32,
+                )
+                for y in range(2):
+                    for k, r in enumerate((top, bottom)):
+                        part = both[k * TILE:(k + 1) * TILE, y * width:(y + 1) * width]
+                        near_push[c, y, k] = main[ACTIVE, y, r, :] * (
+                            main[CONC, y, r, :] * part - main[PUSH_X + c, y, r, :]
+                        )
+        with jax.named_scope("i_packlate"):
+            pack_sides(2)
+            send_sides(2)
+            pack_rows(2)
+            send_ends(2)
+        with jax.named_scope("i_push2"):
             for c in range(2):
                 both = dot_rows(to_blocks, recv[c])
                 for y in range(2):
                     main[PUSH_X + c, y] = main[ACTIVE, y] * (
                         main[CONC, y] * both[:, y * width:(y + 1) * width] - main[PUSH_X + c, y]
                     )
-        with jax.named_scope("i_packlate"):
-            pack_sides(2)
-            send_sides(2)
             pack_flank(2)
             send_flank(2)
-            pack_rows(2)
-            send_ends(2)
 
         def leave(get, u, v):
             dx, dy = u - get(CUR_X), v - get(CUR_Y)
@@ -837,7 +866,7 @@
             tile_loop(groups, 1, lambda g: sweep_main(g, False, True))
         with jax.named_scope("i_sweeps"):
             tile_loop((NSUB - 1) * groups, 1, lambda k: sweep_main(k % groups, True, True))
-        send_rows(0, back, 2, 1, ret, 2, ret_ssem, ret_rsem.at[0])
+        send_rows(0, back, 2, 1, ret, 2, bulk_ssem, bulk_rsem.at[0])
 
         def returned(t):
             r = pl.ds(pl.multiple_of(t * TILE, TILE), TILE)
@@ -854,20 +883,26 @@
             tile_loop(tiles, 4, returned)
             for c in range(2):
                 back[c] = dot_rows(to_slots, forc[c])
+        with jax.named_scope("i_waitmid"):
+            when_inside(-1, 3, mid_rsem.at[0])
+            when_inside(1, 3, mid_rsem.at[1])
+            wait_tiles(2, mid_rsem.at[2])
+            wait_tiles(8, mid_rsem.at[3])
+        unpack_rows(1)
+        unpack_sides(1)
         with jax.named_scope("i_waitlate"):
-            when_inside(-1, 6, later_rsem.at[0])
-            when_inside(1, 6, later_rsem.at[1])
-            wait_tiles(4, later_rsem.at[2])
-            wait_tiles(16, later_rsem.at[3])
+            when_inside(-1, 3, late_rsem.at[0])
+            when_inside(1, 3, late_rsem.at[1])
+            wait_tiles(2, late_rsem.at[2])
+            wait_tiles(8, late_rsem.at[3])
 
         def sweep_strips(stress, velocity):
             sweep_flank(stress, velocity)
             sweep_edge(stress, velocity)
 
         with jax.named_scope("i_edge"):
-            for e in (1, 2):
-                unpack_rows(e)
-                unpack_sides(e)
+            unpack_rows(2)
+            unpack_sides(2)
             sweep_strips(False, True)
             for _ in range(NSUB - 1):
                 sweep_strips(True, True)
@@ -894,10 +929,7 @@
                         ends[c, pl.ds(strip * TILE, TILE), pl.ds(y * width, width)] = jnp.where(
                             held, moved, 0.0
                         )
-            across = lax.dot_general(
-                pieces(flank_back[...], 1), columns,
-                (((1,), (0,)), ((), ())), preferred_element_type=jnp.float32,
-            ).T
+            across = dot_lanes(to_slots, flank_back[...])
             for c in range(2):
                 rest = dot_rows(to_ends, ends[c])
                 for y in range(2):
@@ -908,7 +940,7 @@
                         back[c, r, half] += jnp.where(outer, moved, 0.0) + (
                             rest[t * TILE:(t + 1) * TILE, y * width:(y + 1) * width]
                         )
-            send_rows(0, back, 0, 2, ret, 0, ret_ssem, ret_rsem.at[1])
+            send_rows(0, back, 0, 2, ret, 0, bulk_ssem, bulk_rsem.at[1], "home")
 
         same = jnp.where(diag, 1.0, 0.0).astype(jnp.bfloat16)
         same = jnp.concatenate([same] * 2, axis=1)
@@ -928,7 +960,7 @@
                 theirs = theirs & ((column < NSUB) | (column >= width - NSUB))
                 out[0, c, :, half] = jnp.where(theirs, other, main[c, y])
         wait_bytes(ids.at[pl.ds(0, peers - 1)], ids_ssem)
-        wait_bytes(back, ret_ssem)
+        wait_bytes(back, bulk_ssem)
         when_inside(-1, 6, halo_ssem.at[0])
         when_inside(1, 6, halo_ssem.at[1])
         wait_tiles(4, halo_ssem.at[2])
@@ -967,9 +999,9 @@
             pltpu.VMEM((BX, count), f32),
             pltpu.VMEM((2, 2, BX, count), f32),
             pltpu.VMEM((2, 2 * TILE, cells), f32),
+            pltpu.VMEM((2, 2, 2, TILE, BX), f32),
             *halos, *sides,
-            dma((5,)), dma, dma, dma, dma((2,)), dma, dma((2,)),
-            dma((4,)), dma((4,)), dma((4,)),
+            dma, dma((2,)), dma, dma, dma((4,)), dma((4,)), dma((4,)), dma((4,)),
             pltpu.SemaphoreType.REGULAR,
         ],
         compiler_params=pltpu.CompilerParams(

time: 26.7 us -> 25.8 us (0.966)
  Pallas kernels: 25.8 us -> 25 us
    pallas_call x1, Pallas kernels: 25.8 us -> 25 us  [per_device_kernel(): pl.pallas_call(functools.partial(step_kernel, n_lat, n_lon), out_shape=pl...]
where the time goes in v6:
time: 25.8 us; the launch traced here: 25.7 us
  Pallas kernels  25 us (97%)
  local copies, waits for them, and re-layouts  0.71 us (3%)
    pallas_call x1, Pallas kernels, per_device_kernel(): pl.pallas_call(functools.partial(step_kernel, n_lat, n_lon), out_shape=pl...  25 us
    unnamed x1, local copies, waits for them, and re-layouts  0.71 us

profile of v6, /device:TPU:0, one launch (start us, length us, event | category | flops | bytes accessed | tf_op | source)
XLA Modules:
  0.0 25.7 jit_solution(6872741901516307909)
XLA Ops:
  0.0 25.0 %shard_map.46 = f32[1,2,128,256]{3,2,1,0:T(8,128)S(1)} custom-call(f32[1,7,128,256]{3,2,1,0:T(8,128)} %fields.1, s32[1,128]{1,0:T(1,128)} %bitcast.2, s32[1,128]{1,0:T(1,128)} %bitcast.3, s32[128,256]{1,0:T(8,128)} %land.1), custom_call_target="tpu_custom_call" | custom-call | tf_op jit(solution)/shard_map/pallas_call | solution.py:979
  25.0 0.7 %copy.6 = f32[1,2,128,256]{3,2,1,0:T(8,128)} copy(f32[1,2,128,256]{3,2,1,0:T(8,128)S(1)} %shard_map.46) | data formatting | bytes 524288

commit v7 on v6

--- a/solution.py
+++ b/solution.py
@@ -572,7 +572,13 @@
             def _():
                 wait_tiles(num, sem)
 
-        def unpack_rows(e):
+        def own_rows():
+            for c in range(ROUNDS[0][1]):
+                for y in range(2):
+                    edge[c, 0, y, :, pl.ds(0, width)] = pltpu.roll(main[c, y, top, :], 2, 0)
+                    edge[c, 1, y, :, pl.ds(0, width)] = pltpu.roll(main[c, y, bottom, :], TILE - 2, 0)
+
+        def unpack_rows(e, placed=False):
             lo, num = ROUNDS[e]
             got = rows_got[e]
             for k in range(num // 2):
@@ -580,13 +586,13 @@
                     c, y = lo + 2 * k + i // 2, i % 2
                     north = pltpu.roll(got[0, k], (TILE - 2 * i) % TILE, 0) if i else got[0, k]
                     south = pltpu.roll(got[1, k], TILE - 2 - 2 * i, 0) if i < 3 else got[1, k]
-                    head, foot = main[c, y, top, :], main[c, y, bottom, :]
-                    edge[c, 0, y, :, pl.ds(0, width)] = jnp.where(
-                        sub < 2, north, pltpu.roll(head, 2, 0)
-                    )
-                    edge[c, 1, y, :, pl.ds(0, width)] = jnp.where(
-                        sub >= TILE - 2, south, pltpu.roll(foot, TILE - 2, 0)
-                    )
+                    if placed:
+                        head, foot = (edge[c, strip, y, :, pl.ds(0, width)] for strip in range(2))
+                    else:
+                        head = pltpu.roll(main[c, y, top, :], 2, 0)
+                        foot = pltpu.roll(main[c, y, bottom, :], TILE - 2, 0)
+                    edge[c, 0, y, :, pl.ds(0, width)] = jnp.where(sub < 2, north, head)
+                    edge[c, 1, y, :, pl.ds(0, width)] = jnp.where(sub >= TILE - 2, south, foot)
 
         def unpack_sides(e):
             lo, num = ROUNDS[e]
@@ -621,16 +627,18 @@
                     main[c, y, r, :] = x
                 derive(lambda c: main[c, y, r, :], store)
 
+        def derive_flank():
+            for y in range(2):
+                def store(c, x):
+                    flank[c, y] = x
+                derive(lambda c: flank[c, y], store)
+
         def derive_edges():
             for y in range(2):
                 for strip in range(2):
                     def store(c, x):
                         edge[c, strip, y] = x
                     derive(lambda c: edge[c, strip, y], store)
-
-                def store(c, x):
-                    flank[c, y] = x
-                derive(lambda c: flank[c, y], store)
 
         def sweep_main(g, stress, velocity):
             spots = [
@@ -760,12 +768,10 @@
                     flank[V, y, r, :] = v
 
         with jax.named_scope("i_pack0"):
+            pack_flank(0)
+            send_flank(0)
             pack_rows(0)
             pack_sides(0)
-            send_ends(0)
-            send_sides(0)
-            pack_flank(0)
-            send_flank(0)
         tile_loop(tiles, 2, derive_main)
 
         with jax.named_scope("i_waitids"):
@@ -783,18 +789,13 @@
 
         with jax.named_scope("i_waithalo0"):
             for sems in (halo_ssem, early_rsem):
-                when_inside(-1, 6, sems.at[0])
-                when_inside(1, 6, sems.at[1])
-                wait_tiles(2, sems.at[2])
                 wait_bytes(main.at[0], sems.at[3])
         with jax.named_scope("i_unpack0"):
-            unpack_rows(0)
-            unpack_sides(0)
-            derive_edges()
+            derive_flank()
+            own_rows()
         groups = tiles // GROUP
         with jax.named_scope("i_stress"):
             tile_loop(groups, 1, lambda g: sweep_main(g, True, False))
-            sweep_edge(True, False)
             sweep_flank(True, False)
         by_slot = one_hot[...]
         to_slots = jnp.concatenate([by_slot.astype(jnp.bfloat16)] * 2, axis=1)
@@ -812,6 +813,8 @@
             for y in range(2):
                 main[CUR_X + c, y] = both[:, y * width:(y + 1) * width]
         with jax.named_scope("i_packmid"):
+            send_sides(0)
+            send_ends(0)
             pack_rows(1)
             pack_sides(1)
             send_ends(1)
@@ -883,6 +886,15 @@
             tile_loop(tiles, 4, returned)
             for c in range(2):
                 back[c] = dot_rows(to_slots, forc[c])
+        with jax.named_scope("i_waitearly"):
+            when_inside(-1, 6, early_rsem.at[0])
+            when_inside(1, 6, early_rsem.at[1])
+            wait_tiles(2, early_rsem.at[2])
+        with jax.named_scope("i_early"):
+            unpack_rows(0, True)
+            unpack_sides(0)
+            derive_edges()
+            sweep_edge(True, False)
         with jax.named_scope("i_waitmid"):
             when_inside(-1, 3, mid_rsem.at[0])
             when_inside(1, 3, mid_rsem.at[1])
@@ -961,9 +973,9 @@
                 out[0, c, :, half] = jnp.where(theirs, other, main[c, y])
         wait_bytes(ids.at[pl.ds(0, peers - 1)], ids_ssem)
         wait_bytes(back, bulk_ssem)
-        when_inside(-1, 6, halo_ssem.at[0])
-        when_inside(1, 6, halo_ssem.at[1])
-        wait_tiles(4, halo_ssem.at[2])
+        when_inside(-1, 12, halo_ssem.at[0])
+        when_inside(1, 12, halo_ssem.at[1])
+        wait_tiles(6, halo_ssem.at[2])
         wait_tiles(16, halo_ssem.at[3])
 
 

time: 25.8 us -> 25.5 us (0.988)
  Pallas kernels: 25 us -> 24.7 us
    pallas_call x1, Pallas kernels: 25 us -> 24.7 us  [per_device_kernel(): pl.pallas_call(functools.partial(step_kernel, n_lat, n_lon), out_shape=pl...]
where the time goes in v7:
time: 25.5 us; the launch traced here: 25.4 us
  Pallas kernels  24.7 us (97%)
  local copies, waits for them, and re-layouts  0.71 us (3%)
    pallas_call x1, Pallas kernels, per_device_kernel(): pl.pallas_call(functools.partial(step_kernel, n_lat, n_lon), out_shape=pl...  24.7 us
    unnamed x1, local copies, waits for them, and re-layouts  0.71 us

profile of v7, /device:TPU:0, one launch (start us, length us, event | category | flops | bytes accessed | tf_op | source)
XLA Modules:
  0.0 25.4 jit_solution(8827091565839581573)
XLA Ops:
  0.0 24.7 %shard_map.46 = f32[1,2,128,256]{3,2,1,0:T(8,128)S(1)} custom-call(f32[1,7,128,256]{3,2,1,0:T(8,128)} %fields.1, s32[1,128]{1,0:T(1,128)} %bitcast.2, s32[1,128]{1,0:T(1,128)} %bitcast.3, s32[128,256]{1,0:T(8,128)} %land.1), custom_call_target="tpu_custom_call" | custom-call | tf_op jit(solution)/shard_map/pallas_call | solution.py:991
  24.7 0.7 %copy.6 = f32[1,2,128,256]{3,2,1,0:T(8,128)} copy(f32[1,2,128,256]{3,2,1,0:T(8,128)S(1)} %shard_map.46) | data formatting | bytes 524288

commit v8 on v7

--- a/solution.py
+++ b/solution.py
@@ -262,7 +262,7 @@
     n_lat, n_lon,
     fields, owner_hbm, covered_hbm, land, out,
     surf, open_st, ret, owner, covered, ids, recv, forc, one_hot, back, land_v,
-    main, edge, flank, flank_back, flank_vel, ends, near_push,
+    main, edge, flank, flank_back, flank_vel, ends,
     rows_out0, rows_out1, rows_out2, rows_got0, rows_got1, rows_got2,
     side_out0, side_out1, side_out2, side_got0, side_got1, side_got2,
     bulk_ssem, bulk_rsem, ids_ssem, ids_rsem, halo_ssem, early_rsem, mid_rsem, late_rsem, ready,
@@ -495,18 +495,13 @@
         picker = jnp.where(picked, 1.0, 0.0).astype(jnp.bfloat16)
         picker = jnp.concatenate([picker] * 2, axis=1)
 
-        def end_of(e, c, y, k):
-            if e == 2:
-                return near_push[c - PUSH_X, y, k]
-            return main[c, y, (top, bottom)[k], :]
-
         def pack_rows(e):
             lo, num = ROUNDS[e]
             for k in range(num // 2):
                 ups, downs = zero_tile, zero_tile
                 for i in range(4):
                     c, y = lo + 2 * k + i // 2, i % 2
-                    head, foot = end_of(e, c, y, 0), end_of(e, c, y, 1)
+                    head, foot = main[c, y, top, :], main[c, y, bottom, :]
                     here = (sub >= 2 * i) & (sub < 2 * i + 2)
                     ups = jnp.where(here, pltpu.roll(head, 2 * i, 0) if i else head, ups)
                     downs = jnp.where(here, pltpu.roll(foot, (2 * i + 2) % TILE, 0) if i < 3 else foot, downs)
@@ -518,7 +513,7 @@
             west, east = zero_tile, zero_tile
             for i in range(2 * num):
                 c, y = lo + i // 2, i % 2
-                ends = jnp.where(sub < NSUB, end_of(e, c, y, 0), end_of(e, c, y, 1))
+                ends = jnp.where(sub < NSUB, main[c, y, top, :], main[c, y, bottom, :])
                 slot = i * NSUB
                 mine = (lane >= slot) & (lane < slot + NSUB)
                 west = jnp.where(mine, pltpu.roll(ends, slot, 1) if slot else ends, west)
@@ -641,13 +636,9 @@
                     derive(lambda c: edge[c, strip, y], store)
 
         def sweep_main(g, stress, velocity):
-            spots = [
-                pl.ds(pl.multiple_of((g * GROUP + j) * TILE, TILE), TILE) for j in range(GROUP)
-            ]
-            behind = pl.ds(pl.multiple_of(jnp.maximum(g * GROUP - 1, 0) * TILE, TILE), TILE)
-            ahead = pl.ds(
-                pl.multiple_of(jnp.minimum(g * GROUP + GROUP, tiles - 1) * TILE, TILE), TILE
-            )
+            spots = [pl.ds((g * GROUP + j) * TILE, TILE) for j in range(GROUP)]
+            behind = pl.ds(max(g * GROUP - 1, 0) * TILE, TILE)
+            ahead = pl.ds(min(g * GROUP + GROUP, tiles - 1) * TILE, TILE)
             vels = [[(main[U, y, r, :], main[V, y, r, :]) for y in range(2)] for r in spots]
             stresses = []
             if stress:
@@ -793,9 +784,13 @@
         with jax.named_scope("i_unpack0"):
             derive_flank()
             own_rows()
-        groups = tiles // GROUP
+
+        def sweep_all(stress, velocity):
+            for g in range(tiles // GROUP):
+                sweep_main(g, stress, velocity)
+
         with jax.named_scope("i_stress"):
-            tile_loop(groups, 1, lambda g: sweep_main(g, True, False))
+            sweep_all(True, False)
             sweep_flank(True, False)
         by_slot = one_hot[...]
         to_slots = jnp.concatenate([by_slot.astype(jnp.bfloat16)] * 2, axis=1)
@@ -803,8 +798,6 @@
         to_ends = to_ends.astype(jnp.bfloat16)
         by_block = by_slot.T.astype(jnp.bfloat16)
         to_blocks = jnp.concatenate([by_block] * 2, axis=1)
-        end_blocks = jnp.concatenate([to_blocks[:TILE], to_blocks[count - TILE:]], axis=0)
-        columns = jnp.concatenate([by_block] * 2, axis=0)
 
         with jax.named_scope("i_waitf4"):
             wait_bytes(recv.at[pl.ds(2, 4)], bulk_rsem.at[0])
@@ -833,30 +826,18 @@
             wait_bytes(recv.at[pl.ds(0, 2)], bulk_rsem.at[1])
         with jax.named_scope("i_push"):
             for c in range(2):
-                both = lax.dot_general(
-                    end_blocks, pieces(recv[c], 0), (((1,), (0,)), ((), ())),
-                    preferred_element_type=jnp.float32,
-                )
-                for y in range(2):
-                    for k, r in enumerate((top, bottom)):
-                        part = both[k * TILE:(k + 1) * TILE, y * width:(y + 1) * width]
-                        near_push[c, y, k] = main[ACTIVE, y, r, :] * (
-                            main[CONC, y, r, :] * part - main[PUSH_X + c, y, r, :]
-                        )
-        with jax.named_scope("i_packlate"):
-            pack_sides(2)
-            send_sides(2)
-            pack_rows(2)
-            send_ends(2)
-        with jax.named_scope("i_push2"):
-            for c in range(2):
                 both = dot_rows(to_blocks, recv[c])
                 for y in range(2):
                     main[PUSH_X + c, y] = main[ACTIVE, y] * (
                         main[CONC, y] * both[:, y * width:(y + 1) * width] - main[PUSH_X + c, y]
                     )
+        with jax.named_scope("i_packlate"):
+            pack_sides(2)
+            send_sides(2)
             pack_flank(2)
             send_flank(2)
+            pack_rows(2)
+            send_ends(2)
 
         def leave(get, u, v):
             dx, dy = u - get(CUR_X), v - get(CUR_Y)
@@ -866,9 +847,9 @@
         outer = (lane < NSUB) | (lane >= width - NSUB)
 
         with jax.named_scope("i_vel1"):
-            tile_loop(groups, 1, lambda g: sweep_main(g, False, True))
+            sweep_all(False, True)
         with jax.named_scope("i_sweeps"):
-            tile_loop((NSUB - 1) * groups, 1, lambda k: sweep_main(k % groups, True, True))
+            tile_loop(NSUB - 1, 1, lambda k: sweep_all(True, True))
         send_rows(0, back, 2, 1, ret, 2, bulk_ssem, bulk_rsem.at[0])
 
         def returned(t):
@@ -1011,7 +992,6 @@
             pltpu.VMEM((BX, count), f32),
             pltpu.VMEM((2, 2, BX, count), f32),
             pltpu.VMEM((2, 2 * TILE, cells), f32),
-            pltpu.VMEM((2, 2, 2, TILE, BX), f32),
             *halos, *sides,
             dma, dma((2,)), dma, dma, dma((4,)), dma((4,)), dma((4,)), dma((4,)),
             pltpu.SemaphoreType.REGULAR,

time: 25.5 us -> 25.5 us (level)
  no operation moved by 1% of the time
where the time goes in v8:
time: 25.5 us; the launch traced here: 25.4 us
  Pallas kernels  24.6 us (96%)
  local copies, waits for them, and re-layouts  0.71 us (3%)
    pallas_call x1, Pallas kernels, per_device_kernel(): pl.pallas_call(functools.partial(step_kernel, n_lat, n_lon), out_shape=pl...  24.6 us
    unnamed x1, local copies, waits for them, and re-layouts  0.71 us

profile of v8, /device:TPU:0, one launch (start us, length us, event | category | flops | bytes accessed | tf_op | source)
XLA Modules:
  0.0 25.4 jit_solution(10445826102404395219)
XLA Ops:
  0.0 24.6 %shard_map.46 = f32[1,2,128,256]{3,2,1,0:T(8,128)S(1)} custom-call(f32[1,7,128,256]{3,2,1,0:T(8,128)} %fields.1, s32[1,128]{1,0:T(1,128)} %bitcast.2, s32[1,128]{1,0:T(1,128)} %bitcast.3, s32[128,256]{1,0:T(8,128)} %land.1), custom_call_target="tpu_custom_call" | custom-call | tf_op jit(solution)/shard_map/pallas_call | solution.py:972
  24.7 0.7 %copy.6 = f32[1,2,128,256]{3,2,1,0:T(8,128)} copy(f32[1,2,128,256]{3,2,1,0:T(8,128)S(1)} %shard_map.46) | data formatting | bytes 524288

commit v9 on v8

--- a/solution.py
+++ b/solution.py
@@ -301,8 +301,7 @@
                 for place in along:
                     body(plane * n_lon + place, plane, place)
 
-    def home_first(body):
-        body(0, 0, 0)
+    def away(body):
         for plane in range(n_lat):
             for place in places:
                 if plane:
@@ -328,7 +327,12 @@
                 send_sem=ssem, recv_sem=rsem,
                 device_id=(kind, plane, place), device_id_type=MESH,
             ).start()
-        home_first(body) if part == "home" else each_peer(body, part)
+        if part == "home":
+            body(0, 0, 0)
+        elif part == "away":
+            away(body)
+        else:
+            each_peer(body, part)
 
     def wait_bytes(ref, sem):
         pltpu.make_async_copy(ref, ref, sem).wait()
@@ -933,7 +937,8 @@
                         back[c, r, half] += jnp.where(outer, moved, 0.0) + (
                             rest[t * TILE:(t + 1) * TILE, y * width:(y + 1) * width]
                         )
-            send_rows(0, back, 0, 2, ret, 0, bulk_ssem, bulk_rsem.at[1], "home")
+                send_rows(0, back, c, 1, ret, c, bulk_ssem, bulk_rsem.at[1], "home")
+            send_rows(0, back, 0, 2, ret, 0, bulk_ssem, bulk_rsem.at[1], "away")
 
         same = jnp.where(diag, 1.0, 0.0).astype(jnp.bfloat16)
         same = jnp.concatenate([same] * 2, axis=1)

time: 25.5 us -> 25.5 us (level)
  no operation moved by 1% of the time
where the time goes in v9:
time: 25.5 us; the launch traced here: 25.3 us
  Pallas kernels  24.6 us (96%)
  local copies, waits for them, and re-layouts  0.71 us (3%)
    pallas_call x1, Pallas kernels, per_device_kernel(): pl.pallas_call(functools.partial(step_kernel, n_lat, n_lon), out_shape=pl...  24.6 us
    unnamed x1, local copies, waits for them, and re-layouts  0.71 us

profile of v9, /device:TPU:0, one launch (start us, length us, event | category | flops | bytes accessed | tf_op | source)
XLA Modules:
  0.0 25.3 jit_solution(9192034683319954351)
XLA Ops:
  0.0 24.6 %shard_map.46 = f32[1,2,128,256]{3,2,1,0:T(8,128)S(1)} custom-call(f32[1,7,128,256]{3,2,1,0:T(8,128)} %fields.1, s32[1,128]{1,0:T(1,128)} %bitcast.2, s32[1,128]{1,0:T(1,128)} %bitcast.3, s32[128,256]{1,0:T(8,128)} %land.1), custom_call_target="tpu_custom_call" | custom-call | tf_op jit(solution)/shard_map/pallas_call | solution.py:977
  24.6 0.7 %copy.6 = f32[1,2,128,256]{3,2,1,0:T(8,128)} copy(f32[1,2,128,256]{3,2,1,0:T(8,128)S(1)} %shard_map.46) | data formatting | bytes 524288
